TPU v7x, 32 devices: a whole 2x2x4 slice. The times are simulated.
32 devices in a mesh: mem: 16 (over z, y, x), rep: 2 (over core).
Axes of the slice: x: 2, y: 2, z: 4, core: 2. Of those that a mesh axis runs over, the one named last changes fastest.
Arguments:
- particle_vectors: bfloat16 [64, 131072], P('mem', 'rep'), may hold values from -6 to 6
- observed: bfloat16 [64, 131072], P('mem', 'rep'), may hold values from -24 to 24
- precision: float32 [131072], P('rep'), may hold values from 0.5 to 240, as said below
- entry_projection_matrix: bfloat16 [2, 256, 1024], replicated, may hold values from -0.375 to 0.375
- entry_offsets: float32 [2, 1024], replicated, may hold values from -3 to 3
- exit_projection_matrix: bfloat16 [2, 1024, 256], replicated, may hold values from -0.1875 to 0.1875
- exit_offsets: float32 [2, 256], replicated, may hold values from -3 to 3
Outputs:
- updated: bfloat16 [64, 131072], P('mem', 'rep')
Inputs may be any that keep to these rules, and one draw needn't show every extreme that they name: `precision`: positive precisions.
All inputs are finite; a program needn't handle non-finite values.
Results may differ from a plain program's by a relative error of at most 0.0065.
Values may be sent and summed in bfloat16 or wider, within the bound.
No kernel may reach another device: no remote copies, remote signals or barrier semaphores. Data moves between devices by JAX's collectives and lax.ppermute only.
A program may use at most 64 MiB of HBM per device.

v0:
```python
import jax
import jax.numpy as jnp
from jax import lax
from jax.sharding import PartitionSpec as P

PW = 256
LAYERS = 2


def contract(left, right):
    return lax.dot_general(
        left, right, (((1,), (1,)), ((), ())), preferred_element_type=jnp.float32
    )


def body(
    particle_vectors,
    observed,
    precision,
    entry_projection_matrix,
    entry_offsets,
    exit_projection_matrix,
    exit_offsets,
):
    owned, local_width = particle_vectors.shape
    stream = particle_vectors.reshape(owned * local_width // PW, PW)
    for layer in range(LAYERS):
        pre = (
            jnp.dot(stream, entry_projection_matrix[layer], preferred_element_type=jnp.float32)
            + entry_offsets[layer]
        )
        hidden = jax.nn.silu(pre).astype(jnp.bfloat16)
        stream = (
            stream.astype(jnp.float32)
            + jnp.dot(hidden, exit_projection_matrix[layer], preferred_element_type=jnp.float32)
            + exit_offsets[layer]
        ).astype(jnp.bfloat16)
    particle_outcomes = stream.reshape(owned, local_width)
    resid = (observed.astype(jnp.float32) - particle_outcomes.astype(jnp.float32)).astype(
        jnp.bfloat16
    )
    resid_wide = resid.astype(jnp.float32)
    mem_count = lax.axis_size("mem")
    member_total = owned * mem_count
    state_total = local_width * lax.axis_size("rep")
    misfit_local = jnp.sum(resid_wide * resid_wide * precision)
    damping = lax.psum(misfit_local, ("mem", "rep")) / (member_total * state_total) + 1e-06
    own_states, own_preds, own_resid = (
        lax.all_to_all(particle_vectors, "mem", split_axis=1, concat_axis=0, tiled=True),
        lax.all_to_all(particle_outcomes, "mem", split_axis=1, concat_axis=0, tiled=True),
        lax.all_to_all(resid, "mem", split_axis=1, concat_axis=0, tiled=True),
    )
    block_width = own_states.shape[1]
    prec_block = lax.dynamic_slice_in_dim(
        precision, lax.axis_index("mem") * block_width, block_width
    )
    pred_wide = own_preds.astype(jnp.float32)
    pred_dev = (pred_wide - jnp.mean(pred_wide, axis=0)).astype(jnp.bfloat16)
    state_wide = own_states.astype(jnp.float32)
    state_dev = (state_wide - jnp.mean(state_wide, axis=0)).astype(jnp.bfloat16)
    weighted = (pred_dev.astype(jnp.float32) * prec_block).astype(jnp.bfloat16)
    gram = lax.psum(contract(weighted, pred_dev), ("mem", "rep")) / state_total
    cross = (
        lax.psum_scatter(
            contract(own_resid, weighted), ("mem", "rep"), scatter_dimension=0, tiled=True
        )
        / state_total
    )
    kmat = gram + damping * jnp.eye(member_total, dtype=jnp.float32)
    factor = jnp.linalg.cholesky(kmat)
    middle = jax.scipy.linalg.solve_triangular(factor, cross.T, lower=True)
    solved = jax.scipy.linalg.solve_triangular(factor, middle, lower=True, trans="T")
    mixing = solved.T.astype(jnp.bfloat16)
    fresh = (
        state_wide
        + jnp.dot(
            lax.all_gather(mixing, ("mem", "rep"), axis=0, tiled=True),
            state_dev,
            preferred_element_type=jnp.float32,
        )
    ).astype(jnp.bfloat16)
    return lax.all_to_all(fresh, "mem", split_axis=0, concat_axis=1, tiled=True)


def solution(mesh):
    placed = (P("mem", "rep"), P("mem", "rep"), P("rep"), P(), P(), P(), P())
    return jax.shard_map(
        body, mesh=mesh, in_specs=placed, out_specs=P("mem", "rep"), check_vma=False
    )
```

profile of v0, /device:TPU:0, one launch (start us, length us, event | category | flops | bytes accessed | tf_op | source)
XLA Modules:
  0.0 171.0 jit_solution(16117873625604666661)
XLA Ops:
  0.0 0.8 fusion.32
  0.8 0.8 fusion.33
  1.6 1.4 reshape.69
  3.0 2.5 %fusion.3 = bf16[1024,256]{1,0:T(8,128)(2,1)S(1)} fusion(bf16[1024,256]{1,0:T(8,128)(2,1)S(1)} %reshape.69, f32[1024]{0:T(1024)S(1)} %bitcast.55, f32[256]{0:T(256)S(1)} %bitcast.57, bf16[2,1024,256]{2,1,0:T(8,128)(2,1)S(1)} %copy-done.2, bf16[2,256,1024]{2,1,0:T(8,128)(2,1)} %param.10), kind=kOutput, calls=%fused_computation.12 | convolution fusion | flops 1081081856 | bytes 2626560 | tf_op jit(solution)/shard_map/dot_general | solution.py:35
  5.5 2.5 %fusion.4 = bf16[1024,256]{1,0:T(8,128)(2,1)S(1)} fusion(bf16[1024,256]{1,0:T(8,128)(2,1)S(1)} %fusion.3, f32[1024]{0:T(1024)S(1)} %bitcast.54, f32[256]{0:T(256)S(1)} %bitcast.56, bf16[2,1024,256]{2,1,0:T(8,128)(2,1)S(1)} %copy-done.2, bf16[2,256,1024]{2,1,0:T(8,128)(2,1)} %param.10), kind=kOutput, calls=%fused_computation.13 | convolution fusion | flops 1081081856 | bytes 2626560 | tf_op jit(solution)/shard_map/dot_general | solution.py:35
  8.0 0.2 all_to_all.50
  8.2 1.2 copy.17
  9.4 8.3 %all-to-all-start.1 = ((bf16[4,16,4096]{2,0,1:T(4,128)(2,1)}), bf16[4,16,4096]{2,0,1:T(4,128)(2,1)S(1)}, u32[]{:S(2)}, u32[]{:S(2)}) async-start(bf16[4,16,4096]{2,0,1:T(4,128)(2,1)} %copy.17), calls=%async_computation.1 | async-start | bytes 1048576 | tf_op jit(solution)/shard_map/all_to_all | solution.py:50
  17.8 0.5 reshape.71
  18.3 0.5 copy-done
  18.9 1.9 %multiply_reduce_fusion = (f32[]{:T(128)}, bf16[4,65536]{1,0:T(4,128)(2,1)}) fusion(f32[65536]{0:T(1024)S(1)} %copy-done.1, f32[4,65536]{1,0:T(4,128)S(1)} %reshape.71, bf16[4,65536]{1,0:T(4,128)(2,1)S(1)} %copy-done), kind=kLoop, calls=%fused_computation.18 | loop fusion | flops 1835007 | bytes 2359300 | tf_op jit(solution)/shard_map/reduce_sum | solution.py:46
  20.7 12.1 %all-to-all-done.1 = bf16[4,16,4096]{2,0,1:T(4,128)(2,1)S(1)} async-done(((bf16[4,16,4096]{2,0,1:T(4,128)(2,1)}), bf16[4,16,4096]{2,0,1:T(4,128)(2,1)S(1)}, u32[]{:S(2)}, u32[]{:S(2)}) %all-to-all-start.1) | async-done | bytes 524320 | tf_op jit(solution)/shard_map/all_to_all | solution.py:50
  32.8 3.9 %all-to-all-start.2 = ((bf16[4,16,4096]{2,0,1:T(4,128)(2,1)}), bf16[4,16,4096]{2,0,1:T(4,128)(2,1)S(1)}, u32[]{:S(2)}, u32[]{:S(2)}) async-start(bf16[4,16,4096]{2,0,1:T(4,128)(2,1)} %bitcast.14), calls=%async_computation.2 | async-start | bytes 1048576 | tf_op jit(solution)/shard_map/all_to_all | solution.py:51
  36.8 0.2 convert_reduce_fusion.1
  37.1 0.5 multiply_convert_fusion.2
  37.9 13.4 %all-to-all-done.2 = bf16[4,16,4096]{2,0,1:T(4,128)(2,1)S(1)} async-done(((bf16[4,16,4096]{2,0,1:T(4,128)(2,1)}), bf16[4,16,4096]{2,0,1:T(4,128)(2,1)S(1)}, u32[]{:S(2)}, u32[]{:S(2)}) %all-to-all-start.2) | async-done | bytes 524320 | tf_op jit(solution)/shard_map/all_to_all | solution.py:51
  51.2 3.9 %all-to-all-start = ((bf16[4,16,4096]{2,0,1:T(4,128)(2,1)}), bf16[4,16,4096]{2,0,1:T(4,128)(2,1)S(1)}, u32[]{:S(2)}, u32[]{:S(2)}) async-start(bf16[4,16,4096]{2,0,1:T(4,128)(2,1)} %bitcast), calls=%async_computation | async-start | bytes 1048576 | tf_op jit(solution)/shard_map/all_to_all | solution.py:49
  55.2 0.3 fusion.34
  55.5 0.3 fusion.35
  55.8 42.0 %all-reduce.1 = (f32[64,64]{1,0:T(8,128)S(1)}, f32[]{:T(128)}, f32[64,64]{1,0:T(8,128)S(1)}) all-reduce(f32[64,64]{1,0:T(8,128)S(1)} %fusion.34, f32[]{:T(128)} %get-tuple-element.8, f32[64,64]{1,0:T(8,128)S(1)} %fusion.35), channel_id=1, replica_groups=mesh['mem'=16,'rep'=2] {'mem','rep'}, use_global_device_ids=true, to_apply=%region_1.2 | all-reduce | flops 8193 | bytes 65544 | tf_op jit(solution)/shard_map/psum | solution.py:62
  98.6 5.8 %cholesky.16 = f32[64,64]{1,0:T(8,128)S(1)} custom-call(f32[64,64]{1,0:T(8,128)S(1)} %fusion.25), custom_call_target="Cholesky" | custom-call | tf_op jit(solution)/shard_map/jit(cholesky)/cholesky | solution.py:70
  104.5 0.6 compare_reduce_fusion
  105.2 0.7 fusion.21
  105.8 4.9 %custom-call.10 = f32[1,64,64]{1,2,0:T(8,128)S(1)} custom-call(f32[1,64,64]{2,1,0:T(8,128)S(1)} %fusion.21), custom_call_target="InvertDiagBlocksLowerTriangular" | custom-call | tf_op jit(solution)/shard_map/jit(_solve_triangular)/triangular_solve | solution.py:72
  110.9 0.2 fusion.5
  111.0 39.9 %all-gather = bf16[32,2,64]{2,1,0:T(2,128)(2,1)S(1)} all-gather(bf16[1,2,64]{2,1,0:T(2,128)(2,1)S(1)} %fusion.5), channel_id=1, replica_groups=mesh['mem'=16,'rep'=2] {'mem','rep'}, dimensions={0}, use_global_device_ids=true | all-gather | bytes 8448 | tf_op jit(solution)/shard_map/all_gather | solution.py:77
  151.0 0.4 reshape.70
  151.4 0.2 convert_reduce_fusion
  151.6 0.3 fusion
  151.9 0.2 all_to_all.56
  152.1 18.1 %all_to_all.64 = bf16[16,4,4096]{2,1,0:T(4,128)(2,1)S(1)} all-to-all(bf16[16,4,4096]{2,1,0:T(4,128)(2,1)S(1)} %all_to_all.56), channel_id=1, replica_groups=mesh['mem'=16,'rep'=2] {'mem'}, dimensions={0} | all-to-all | bytes 1048576 | tf_op jit(solution)/shard_map/all_to_all | solution.py:82
  170.2 0.8 copy.22
  (19 shorter events, 0.8 us)
Async XLA Ops:
  0.0 3.0 %copy-start.2 = (bf16[2,1024,256]{2,1,0:T(8,128)(2,1)S(1)}, bf16[2,1024,256]{2,1,0:T(8,128)(2,1)}, u32[]{:S(2)}) copy-start(bf16[2,1024,256]{2,1,0:T(8,128)(2,1)} %param.12) | copy-start | bytes 3145732
  9.4 23.4 %all-to-all-start.1 = ((bf16[4,16,4096]{2,0,1:T(4,128)(2,1)}), bf16[4,16,4096]{2,0,1:T(4,128)(2,1)S(1)}, u32[]{:S(2)}, u32[]{:S(2)}) async-start(bf16[4,16,4096]{2,0,1:T(4,128)(2,1)} %copy.17), calls=%async_computation.1 | async-start | bytes 1048576 | tf_op jit(solution)/shard_map/all_to_all | solution.py:50
  17.8 1.0 copy-start
  17.8 1.1 copy-start.1
  20.7 16.3 %dynamic-slice-start = ((f32[65536]{0:T(1024)}, s32[]{:T(128)}), f32[4096]{0:T(1024)S(1)}, s32[]{:S(2)}) async-start(f32[65536]{0:T(1024)} %param.9, s32[]{:T(128)} %select_n.7), calls=%async_computation.4 | async-start | bytes 33280 | tf_op jit(solution)/shard_map/dynamic_slice | solution.py:54
  32.8 18.4 %all-to-all-start.2 = ((bf16[4,16,4096]{2,0,1:T(4,128)(2,1)}), bf16[4,16,4096]{2,0,1:T(4,128)(2,1)S(1)}, u32[]{:S(2)}, u32[]{:S(2)}) async-start(bf16[4,16,4096]{2,0,1:T(4,128)(2,1)} %bitcast.14), calls=%async_computation.2 | async-start | bytes 1048576 | tf_op jit(solution)/shard_map/all_to_all | solution.py:51
  51.2 99.7 %all-to-all-start = ((bf16[4,16,4096]{2,0,1:T(4,128)(2,1)}), bf16[4,16,4096]{2,0,1:T(4,128)(2,1)S(1)}, u32[]{:S(2)}, u32[]{:S(2)}) async-start(bf16[4,16,4096]{2,0,1:T(4,128)(2,1)} %bitcast), calls=%async_computation | async-start | bytes 1048576 | tf_op jit(solution)/shard_map/all_to_all | solution.py:49
where the time goes:
time: 172 us; the launch traced here: 171 us
  blocking collectives  100 us (58%)
  waiting for transfers between devices  25.5 us (15%)
  starting transfers between devices  16.2 us (9%)
  other arithmetic  15.1 us (9%)
  local copies, waits for them, and re-layouts  7.34 us (4%)
  matrix products  6.07 us (4%)
    psum x1, blocking collectives, body(): gram = lax.psum(contract(weighted, pred_dev), ('mem', 'rep')) / state_total  42 us
    all_gather x1, blocking collectives, body(): lax.all_gather(mixing, ('mem', 'rep'), axis=0, tiled=True)  39.9 us
    all_to_all x1, blocking collectives, body(): return lax.all_to_all(fresh, 'mem', split_axis=0, concat_axis=1, tiled=True)  18.1 us
    all_to_all x1, waiting for transfers between devices, body(): lax.all_to_all(resid, 'mem', split_axis=1, concat_axis=0, tiled=True)  13.4 us
    all_to_all x1, waiting for transfers between devices, body(): lax.all_to_all(particle_outcomes, 'mem', split_axis=1, concat_axis=0, til...  12.1 us
    all_to_all x1, starting transfers between devices, body(): lax.all_to_all(particle_outcomes, 'mem', split_axis=1, concat_axis=0, til...  8.34 us
    another operation x3, other arithmetic, body(): factor = jnp.linalg.cholesky(kmat)  6.52 us
    another operation x2, other arithmetic, body(): jax.scipy.linalg.solve_triangular(factor, middle, lower=True, trans='T')  5.55 us
  transfers between devices with their start and end apart: 3, of which 2 were waited for; matrix products, arithmetic and copies ran while one was open for 10% of the time, Pallas kernels for 0%

commit v1 on v0

v1 whole, which is shorter than its diff:
```python
import jax
import jax.numpy as jnp
from jax import lax
from jax.sharding import PartitionSpec as P

PW = 256
LAYERS = 2


def contract(left, right):
    return lax.dot_general(
        left, right, (((1,), (1,)), ((), ())), preferred_element_type=jnp.float32
    )


def to_block(value):
    return lax.all_to_all(value, "mem", split_axis=1, concat_axis=0, tiled=True)


def total_over_devices(value):
    for axis in ("rep", "mem"):
        size = lax.axis_size(axis)
        if size & (size - 1):
            value = lax.psum(value, axis)
            continue
        bit = 1
        while bit < size:
            mask = bit ^ (bit >> 1) if bit * 2 == size else bit
            value = value + lax.ppermute(value, axis, [(i, i ^ mask) for i in range(size)])
            bit *= 2
    return value


def forecast(states, entry_w, entry_b, exit_w, exit_b):
    members, width = states.shape
    stream = states.reshape(members, width // PW, PW).transpose(1, 0, 2).reshape(-1, PW)
    for layer in range(LAYERS):
        pre = jnp.dot(stream, entry_w[layer], preferred_element_type=jnp.float32) + entry_b[layer]
        hidden = jax.nn.silu(pre).astype(jnp.bfloat16)
        stream = (
            stream.astype(jnp.float32)
            + jnp.dot(hidden, exit_w[layer], preferred_element_type=jnp.float32)
            + exit_b[layer]
        ).astype(jnp.bfloat16)
    return stream.reshape(width // PW, members, PW).transpose(1, 0, 2).reshape(members, width)


def body(
    particle_vectors,
    observed,
    precision,
    entry_projection_matrix,
    entry_offsets,
    exit_projection_matrix,
    exit_offsets,
):
    state_total = particle_vectors.shape[1] * lax.axis_size("rep")
    own_states = to_block(particle_vectors)
    own_obs = to_block(observed)
    member_total, block_width = own_states.shape
    prec_block = lax.dynamic_slice_in_dim(
        precision, lax.axis_index("mem") * block_width, block_width
    )
    own_preds = forecast(
        own_states, entry_projection_matrix, entry_offsets, exit_projection_matrix, exit_offsets
    )
    pred_wide = own_preds.astype(jnp.float32)
    pred_dev = (pred_wide - jnp.mean(pred_wide, axis=0)).astype(jnp.bfloat16)
    weighted = (pred_dev.astype(jnp.float32) * prec_block).astype(jnp.bfloat16)
    state_wide = own_states.astype(jnp.float32)
    state_dev = (state_wide - jnp.mean(state_wide, axis=0)).astype(jnp.bfloat16)
    gram = contract(weighted, pred_dev)
    resid = (own_obs.astype(jnp.float32) - pred_wide).astype(jnp.bfloat16)
    resid_wide = resid.astype(jnp.float32)
    misfit = jnp.sum(resid_wide * resid_wide * prec_block)
    cross_t = contract(weighted, resid)
    eye = jnp.eye(member_total, dtype=jnp.float32)
    joined = jnp.concatenate([gram + (misfit / member_total) * eye, cross_t], axis=1)
    joined = total_over_devices(joined) / state_total
    kmat = joined[:, :member_total] + 1e-06 * eye
    factor = jnp.linalg.cholesky(kmat)
    middle = jax.scipy.linalg.solve_triangular(factor, joined[:, member_total:], lower=True)
    solved = jax.scipy.linalg.solve_triangular(factor, middle, lower=True, trans="T")
    mixing = solved.T.astype(jnp.bfloat16)
    fresh = (
        state_wide + jnp.dot(mixing, state_dev, preferred_element_type=jnp.float32)
    ).astype(jnp.bfloat16)
    return lax.all_to_all(fresh, "mem", split_axis=0, concat_axis=1, tiled=True)


def solution(mesh):
    placed = (P("mem", "rep"), P("mem", "rep"), P("rep"), P(), P(), P(), P())
    return jax.shard_map(
        body, mesh=mesh, in_specs=placed, out_specs=P("mem", "rep"), check_vma=False
    )
```

time: 172 us -> 93.5 us (0.54)
  blocking collectives: 100 us -> 15.1 us
  waiting for transfers between devices: 25.5 us -> 30.1 us
    psum x1 -> x0, blocking collectives: 42 us -> none  [body(): gram = lax.psum(contract(weighted, pred_dev), ('mem', 'rep')) / state_total]
    all_gather x1 -> x0, blocking collectives: 39.9 us -> none  [body(): lax.all_gather(mixing, ('mem', 'rep'), axis=0, tiled=True)]
    ppermute x0 -> x5, waiting for transfers between devices: none -> 13.4 us  [total_over_devices(): lax.ppermute(value, axis, [(i, i ^ mask) for i in range(size)])]
    all_to_all x3 -> x2, waiting for transfers between devices: 25.5 us -> 16.7 us  [to_block(): return lax.all_to_all(value, 'mem', split_axis=1, concat_axis=0, tiled=True)]
    ppermute x0 -> x5, starting transfers between devices: none -> 4.61 us  [total_over_devices(): lax.ppermute(value, axis, [(i, i ^ mask) for i in range(size)])]
    all_to_all x3 -> x2, starting transfers between devices: 16.2 us -> 12.4 us  [to_block(): return lax.all_to_all(value, 'mem', split_axis=1, concat_axis=0, tiled=True)]
    all_to_all x1, blocking collectives: 18.1 us -> 15.1 us  [body(): return lax.all_to_all(fresh, 'mem', split_axis=0, concat_axis=1, tiled=True)]
    convert_element_type x3, local copies, waits for them, and re-layouts: 0.77 us -> 3.42 us  [the longest x2 3.3 us: body(): pred_wide = own_preds.astype(jnp.float32)]
  transfers between devices with their start and end apart: 3 -> 7, of which waited for: 2 -> 7; matrix products, arithmetic and copies ran while one was open for 10% -> 14% of each run, Pallas kernels for 0% -> 0%
where the time goes in v1:
time: 93.5 us; the launch traced here: 93 us
  waiting for transfers between devices  30.1 us (32%)
  starting transfers between devices  17 us (18%)
  other arithmetic  15.7 us (17%)
  blocking collectives  15.1 us (16%)
  local copies, waits for them, and re-layouts  7.54 us (8%)
  matrix products  6.7 us (7%)
    all_to_all x2, waiting for transfers between devices, to_block(): return lax.all_to_all(value, 'mem', split_axis=1, concat_axis=0, tiled=True)  16.7 us
    all_to_all x1, blocking collectives, body(): return lax.all_to_all(fresh, 'mem', split_axis=0, concat_axis=1, tiled=True)  15.1 us
    ppermute x5, waiting for transfers between devices, total_over_devices(): lax.ppermute(value, axis, [(i, i ^ mask) for i in range(size)])  13.4 us
    all_to_all x2, starting transfers between devices, to_block(): return lax.all_to_all(value, 'mem', split_axis=1, concat_axis=0, tiled=True)  12.4 us
    another operation x3, other arithmetic, body(): factor = jnp.linalg.cholesky(kmat)  6.52 us
    another operation x2, other arithmetic, body(): jax.scipy.linalg.solve_triangular(factor, middle, lower=True, trans='T')  5.55 us
    dot_general x2, matrix products, forecast(): jnp.dot(hidden, exit_w[layer], preferred_element_type=jnp.float32)  5.23 us
    ppermute x5, starting transfers between devices, total_over_devices(): lax.ppermute(value, axis, [(i, i ^ mask) for i in range(size)])  4.61 us
  transfers between devices with their start and end apart: 7, of which 7 were waited for; matrix products, arithmetic and copies ran while one was open for 14% of the time, Pallas kernels for 0%

profile of v1, /device:TPU:0, one launch (start us, length us, event | category | flops | bytes accessed | tf_op | source)
XLA Modules:
  0.0 93.0 jit_solution(8597595605520606507)
XLA Ops:
  0.0 8.5 %all-to-all-start = ((bf16[4,16,4096]{2,0,1:T(4,128)(2,1)}), bf16[4,16,4096]{2,0,1:T(4,128)(2,1)S(1)}, u32[]{:S(2)}, u32[]{:S(2)}) async-start(bf16[4,16,4096]{2,0,1:T(4,128)(2,1)} %bitcast.79), calls=%async_computation | async-start | bytes 1048576 | tf_op jit(solution)/shard_map/all_to_all | solution.py:17
  8.5 0.7 dynamic_slice.3
  9.3 14.3 %all-to-all-done = bf16[4,16,4096]{2,0,1:T(4,128)(2,1)S(1)} async-done(((bf16[4,16,4096]{2,0,1:T(4,128)(2,1)}), bf16[4,16,4096]{2,0,1:T(4,128)(2,1)S(1)}, u32[]{:S(2)}, u32[]{:S(2)}) %all-to-all-start) | async-done | bytes 524320 | tf_op jit(solution)/shard_map/all_to_all | solution.py:17
  23.6 3.9 %all-to-all-start.1 = ((bf16[4,16,4096]{2,0,1:T(4,128)(2,1)}), bf16[4,16,4096]{2,0,1:T(4,128)(2,1)S(1)}, u32[]{:S(2)}, u32[]{:S(2)}) async-start(bf16[4,16,4096]{2,0,1:T(4,128)(2,1)} %bitcast.15), calls=%async_computation.1 | async-start | bytes 1048576 | tf_op jit(solution)/shard_map/all_to_all | solution.py:17
  27.5 0.4 reshape.83
  28.1 2.6 %fusion.3 = bf16[1024,256]{1,0:T(8,128)(2,1)S(1)} fusion(bf16[1024,256]{1,0:T(8,128)(2,1)S(1)} %bitcast.80, f32[1024]{0:T(1024)S(1)} %bitcast.82, f32[256]{0:T(256)S(1)} %bitcast.84, bf16[2,1024,256]{2,1,0:T(8,128)(2,1)} %param.12, bf16[2,256,1024]{2,1,0:T(8,128)(2,1)} %param.10), kind=kOutput, calls=%fused_computation.8 | convolution fusion | flops 1081081856 | bytes 2626560 | tf_op jit(solution)/shard_map/dot_general | solution.py:42
  30.7 2.6 %bitcast_convert_fusion.1 = f32[16,64,256]{2,1,0:T(8,128)S(1)} fusion(f32[256]{0:T(256)S(1)} %bitcast.83, bf16[2,1024,256]{2,1,0:T(8,128)(2,1)} %param.12, bf16[1024,256]{1,0:T(8,128)(2,1)S(1)} %fusion.3, f32[1024]{0:T(1024)S(1)} %bitcast.81, bf16[2,256,1024]{2,1,0:T(8,128)(2,1)} %param.10), kind=kOutput, calls=%fused_computation.55 | convolution fusion | flops 1081344000 | bytes 3150848 | tf_op jit(solution)/shard_map/dot_general | solution.py:42
  33.3 1.6 %copy.29 = f32[16,64,256]{2,0,1:T(8,128)} copy(f32[16,64,256]{2,1,0:T(8,128)S(1)} %bitcast_convert_fusion.1) | data formatting | bytes 2097152 | tf_op jit(solution)/shard_map/convert_element_type | solution.py:67
  34.9 1.7 %reshape.86 = f32[16,4,4096]{2,1,0:T(4,128)S(1)} reshape(f32[64,16,256]{2,1,0:T(8,128)} %bitcast.74) | data formatting | bytes 2097152 | tf_op jit(solution)/shard_map/convert_element_type | solution.py:67
  36.6 0.5 fusion.30
  37.2 1.4 %multiply_convert_fusion.2 = (bf16[64,16,256]{2,1,0:T(8,128)(2,1)S(1)}, bf16[64,16,256]{2,1,0:T(8,128)(2,1)}) fusion(f32[16,256]{1,0:T(8,128)S(1)} %mul.50, f32[16,256]{1,0:T(8,128)S(1)} %broadcast_multiply_fusion.1, f32[16,64,256]{2,1,0:T(8,128)S(1)} %bitcast_convert_fusion.1), kind=kLoop, calls=%fused_computation.18 | loop fusion | flops 1310720 | bytes 2129920 | tf_op jit(solution)/shard_map/convert_element_type | solution.py:69
  38.6 0.8 copy-done
  39.5 2.4 %all-to-all-done.1 = bf16[4,16,4096]{2,0,1:T(4,128)(2,1)S(1)} async-done(((bf16[4,16,4096]{2,0,1:T(4,128)(2,1)}), bf16[4,16,4096]{2,0,1:T(4,128)(2,1)S(1)}, u32[]{:S(2)}, u32[]{:S(2)}) %all-to-all-start.1) | async-done | bytes 524320 | tf_op jit(solution)/shard_map/all_to_all | solution.py:17
  41.9 1.1 %multiply_reduce_fusion = (f32[]{:T(128)}, bf16[16,4,4096]{2,1,0:T(4,128)(2,1)S(1)}) fusion(f32[4096]{0:T(1024)S(1)} %dynamic_slice.3, f32[16,4,4096]{2,1,0:T(4,128)S(1)} %reshape.86, bf16[4,16,4096]{2,0,1:T(4,128)(2,1)S(1)} %all-to-all-done.1), kind=kLoop, calls=%fused_computation.17 | loop fusion | flops 1835007 | bytes 2113540 | tf_op jit(solution)/shard_map/reduce_sum | solution.py:75
  43.8 0.3 copy-done.1
  44.3 0.4 fusion.5
  45.1 1.2 %collective-permute-done = f32[64,128]{1,0:T(8,128)S(1)} collective-permute-done((f32[64,128]{1,0:T(8,128)S(1)}, f32[64,128]{1,0:T(8,128)S(1)}, u32[]{:S(2)}, u32[]{:S(2)}) %collective-permute-start) | collective-permute-done | bytes 32800 | tf_op jit(solution)/shard_map/ppermute | solution.py:29
  46.4 0.6 collective-permute-start.1
  46.9 3.4 %collective-permute-done.1 = f32[64,128]{1,0:T(8,128)S(1)} collective-permute-done((f32[64,128]{1,0:T(8,128)S(1)}, f32[64,128]{1,0:T(8,128)S(1)}, u32[]{:S(2)}, u32[]{:S(2)}) %collective-permute-start.1) | collective-permute-done | bytes 32800 | tf_op jit(solution)/shard_map/ppermute | solution.py:29
  50.3 0.9 collective-permute-start.2
  51.3 2.9 %collective-permute-done.2 = f32[64,128]{1,0:T(8,128)S(1)} collective-permute-done((f32[64,128]{1,0:T(8,128)S(1)}, f32[64,128]{1,0:T(8,128)S(1)}, u32[]{:S(2)}, u32[]{:S(2)}) %collective-permute-start.2) | collective-permute-done | bytes 32800 | tf_op jit(solution)/shard_map/ppermute | solution.py:29
  54.2 1.3 %collective-permute-start.3 = (f32[64,128]{1,0:T(8,128)S(1)}, f32[64,128]{1,0:T(8,128)S(1)}, u32[]{:S(2)}, u32[]{:S(2)}) collective-permute-start(f32[64,128]{1,0:T(8,128)S(1)} %add.115), channel_id=1, source_target_pairs={{0,8},{2,10},{4,12},{6,14},{8,0},{10,2},{12,4},{14,6},{16,24},{18,... | collective-permute-start | bytes 98312 | tf_op jit(solution)/shard_map/ppermute | solution.py:29
  55.7 2.4 %collective-permute-done.3 = f32[64,128]{1,0:T(8,128)S(1)} collective-permute-done((f32[64,128]{1,0:T(8,128)S(1)}, f32[64,128]{1,0:T(8,128)S(1)}, u32[]{:S(2)}, u32[]{:S(2)}) %collective-permute-start.3) | collective-permute-done | bytes 32800 | tf_op jit(solution)/shard_map/ppermute | solution.py:29
  58.1 1.8 %collective-permute-start.4 = (f32[64,128]{1,0:T(8,128)S(1)}, f32[64,128]{1,0:T(8,128)S(1)}, u32[]{:S(2)}, u32[]{:S(2)}) collective-permute-start(f32[64,128]{1,0:T(8,128)S(1)} %add.116), channel_id=1, source_target_pairs={{0,24},{2,26},{4,28},{6,30},{8,16},{10,18},{12,20},{14,22},{16,8},... | collective-permute-start | bytes 98312 | tf_op jit(solution)/shard_map/ppermute | solution.py:29
  60.0 0.4 reshape.85
  60.3 3.5 %collective-permute-done.4 = f32[64,128]{1,0:T(8,128)S(1)} collective-permute-done((f32[64,128]{1,0:T(8,128)S(1)}, f32[64,128]{1,0:T(8,128)S(1)}, u32[]{:S(2)}, u32[]{:S(2)}) %collective-permute-start.4) | collective-permute-done | bytes 32800 | tf_op jit(solution)/shard_map/ppermute | solution.py:29
  64.0 5.8 %cholesky.17 = f32[64,64]{1,0:T(8,128)S(1)} custom-call(f32[64,64]{1,0:T(8,128)S(1)} %fusion.27), custom_call_target="Cholesky" | custom-call | tf_op jit(solution)/shard_map/jit(cholesky)/cholesky | solution.py:81
  69.9 0.6 compare_reduce_fusion
  70.5 0.7 fusion.22
  71.2 4.9 %custom-call.10 = f32[1,64,64]{1,2,0:T(8,128)S(1)} custom-call(f32[1,64,64]{2,1,0:T(8,128)S(1)} %fusion.22), custom_call_target="InvertDiagBlocksLowerTriangular" | custom-call | tf_op jit(solution)/shard_map/jit(_solve_triangular)/triangular_solve | solution.py:83
  77.1 15.1 %all_to_all.48 = bf16[16,4,4096]{2,1,0:T(4,128)(2,1)S(1)} all-to-all(bf16[16,4,4096]{2,1,0:T(4,128)(2,1)S(1)} %all_to_all.41), channel_id=1, replica_groups=mesh['mem'=16,'rep'=2] {'mem'}, dimensions={0} | all-to-all | bytes 1048576 | tf_op jit(solution)/shard_map/all_to_all | solution.py:88
  92.2 0.8 copy.31
  (34 shorter events, 2.6 us)
Async XLA Ops:
  0.0 9.2 %copy-start.4 = (f32[2,256]{1,0:T(2,128)S(1)}, f32[2,256]{1,0:T(2,128)}, u32[]{:S(2)}) copy-start(f32[2,256]{1,0:T(2,128)} %param.13) | copy-start | bytes 6148
  0.0 9.2 %copy-start.3 = (f32[2,1024]{1,0:T(2,128)S(1)}, f32[2,1024]{1,0:T(2,128)}, u32[]{:S(2)}) copy-start(f32[2,1024]{1,0:T(2,128)} %param.11) | copy-start | bytes 24580
  0.0 23.6 %all-to-all-start = ((bf16[4,16,4096]{2,0,1:T(4,128)(2,1)}), bf16[4,16,4096]{2,0,1:T(4,128)(2,1)S(1)}, u32[]{:S(2)}, u32[]{:S(2)}) async-start(bf16[4,16,4096]{2,0,1:T(4,128)(2,1)} %bitcast.79), calls=%async_computation | async-start | bytes 1048576 | tf_op jit(solution)/shard_map/all_to_all | solution.py:17
  23.6 18.4 %all-to-all-start.1 = ((bf16[4,16,4096]{2,0,1:T(4,128)(2,1)}), bf16[4,16,4096]{2,0,1:T(4,128)(2,1)S(1)}, u32[]{:S(2)}, u32[]{:S(2)}) async-start(bf16[4,16,4096]{2,0,1:T(4,128)(2,1)} %bitcast.15), calls=%async_computation.1 | async-start | bytes 1048576 | tf_op jit(solution)/shard_map/all_to_all | solution.py:17
  38.6 0.8 copy-start
  43.1 1.0 %copy-start.1 = (bf16[64,16,256]{2,1,0:T(8,128)(2,1)S(1)}, bf16[64,16,256]{2,1,0:T(8,128)(2,1)}, u32[]{:S(2)}) copy-start(bf16[64,16,256]{2,1,0:T(8,128)(2,1)} %copy-done) | copy-start | bytes 1572868
  43.1 1.2 %copy-start.2 = (bf16[64,16,256]{2,1,0:T(8,128)(2,1)S(1)}, bf16[64,16,256]{2,1,0:T(8,128)(2,1)}, u32[]{:S(2)}) copy-start(bf16[64,16,256]{2,1,0:T(8,128)(2,1)} %get-tuple-element.8) | copy-start | bytes 1572868
  45.1 1.2 %collective-permute-start = (f32[64,128]{1,0:T(8,128)S(1)}, f32[64,128]{1,0:T(8,128)S(1)}, u32[]{:S(2)}, u32[]{:S(2)}) collective-permute-start(f32[64,128]{1,0:T(8,128)S(1)} %pad_maximum_fusion), channel_id=1, source_target_pairs={{0,1},{1,0},{2,3},{3,2},{4,5},{5,4},{6,7},{7,6},{8,9},{9,8},{10,11... | collective-permute-start | bytes 98312 | tf_op jit(solution)/shard_map/ppermute | solution.py:29
  46.4 3.9 %collective-permute-start.1 = (f32[64,128]{1,0:T(8,128)S(1)}, f32[64,128]{1,0:T(8,128)S(1)}, u32[]{:S(2)}, u32[]{:S(2)}) collective-permute-start(f32[64,128]{1,0:T(8,128)S(1)} %fusion.41), channel_id=1, source_target_pairs={{0,2},{2,0},{4,6},{6,4},{8,10},{10,8},{12,14},{14,12},{16,18},{18,... | collective-permute-start | bytes 98312 | tf_op jit(solution)/shard_map/ppermute | solution.py:29
  50.3 3.9 %collective-permute-start.2 = (f32[64,128]{1,0:T(8,128)S(1)}, f32[64,128]{1,0:T(8,128)S(1)}, u32[]{:S(2)}, u32[]{:S(2)}) collective-permute-start(f32[64,128]{1,0:T(8,128)S(1)} %add.114), channel_id=1, source_target_pairs={{0,4},{2,6},{4,0},{6,2},{8,12},{10,14},{12,8},{14,10},{16,20},{18,... | collective-permute-start | bytes 98312 | tf_op jit(solution)/shard_map/ppermute | solution.py:29
  54.2 3.9 %collective-permute-start.3 = (f32[64,128]{1,0:T(8,128)S(1)}, f32[64,128]{1,0:T(8,128)S(1)}, u32[]{:S(2)}, u32[]{:S(2)}) collective-permute-start(f32[64,128]{1,0:T(8,128)S(1)} %add.115), channel_id=1, source_target_pairs={{0,8},{2,10},{4,12},{6,14},{8,0},{10,2},{12,4},{14,6},{16,24},{18,... | collective-permute-start | bytes 98312 | tf_op jit(solution)/shard_map/ppermute | solution.py:29
  58.1 5.7 %collective-permute-start.4 = (f32[64,128]{1,0:T(8,128)S(1)}, f32[64,128]{1,0:T(8,128)S(1)}, u32[]{:S(2)}, u32[]{:S(2)}) collective-permute-start(f32[64,128]{1,0:T(8,128)S(1)} %add.116), channel_id=1, source_target_pairs={{0,24},{2,26},{4,28},{6,30},{8,16},{10,18},{12,20},{14,22},{16,8},... | collective-permute-start | bytes 98312 | tf_op jit(solution)/shard_map/ppermute | solution.py:29

commit v2 on v1

--- a/solution.py
+++ b/solution.py
@@ -1,10 +1,16 @@
 import jax
 import jax.numpy as jnp
 from jax import lax
+from jax.experimental import pallas as pl
+from jax.experimental.pallas import tpu as pltpu
 from jax.sharding import PartitionSpec as P
 
 PW = 256
 LAYERS = 2
+SUB = 8
+LANES = 128
+CHUNK = 512
+VMEM_LIMIT = 8 * 1024 * 1024
 
 
 def contract(left, right):
@@ -18,17 +24,19 @@
 
 
 def total_over_devices(value):
+    other = jnp.zeros_like(value)
     for axis in ("rep", "mem"):
         size = lax.axis_size(axis)
         if size & (size - 1):
-            value = lax.psum(value, axis)
+            value, other = lax.psum(value + other, axis), jnp.zeros_like(value)
             continue
         bit = 1
         while bit < size:
             mask = bit ^ (bit >> 1) if bit * 2 == size else bit
-            value = value + lax.ppermute(value, axis, [(i, i ^ mask) for i in range(size)])
+            value = value + other
+            other = lax.ppermute(value, axis, [(i, i ^ mask) for i in range(size)])
             bit *= 2
-    return value
+    return value, other
 
 
 def forecast(states, entry_w, entry_b, exit_w, exit_b):
@@ -43,6 +51,81 @@
             + exit_b[layer]
         ).astype(jnp.bfloat16)
     return stream.reshape(width // PW, members, PW).transpose(1, 0, 2).reshape(members, width)
+
+
+def eliminate(blocks, first):
+    shape = blocks[0].shape
+    row = lax.broadcasted_iota(jnp.int32, shape, 0)
+    for kb in range(len(blocks)):
+        lo = first + kb * SUB
+        cols = [
+            [jnp.broadcast_to(block[:, lo + j : lo + j + 1], shape) for j in range(SUB)]
+            for block in blocks
+        ]
+        pivot = blocks[kb]
+        own = list(cols[kb])
+        for p in range(SUB):
+            factor = own[p]
+            inv = 1.0 / factor[p : p + 1, :]
+            line = pivot[p : p + 1, :] * inv
+            pivot = jnp.where(row == p, line, pivot - factor * line)
+            for j in range(p + 1, SUB):
+                line = own[j][p : p + 1, :] * inv
+                own[j] = jnp.where(row == p, line, own[j] - factor * line)
+        after = []
+        for i, block in enumerate(blocks):
+            if i == kb:
+                after.append(pivot)
+                continue
+            terms = [cols[i][j] * pivot[j : j + 1, :] for j in range(SUB)]
+            while len(terms) > 1:
+                terms = [terms[t] + terms[t + 1] for t in range(0, len(terms), 2)]
+            after.append(block - terms[0])
+        blocks = after
+    return blocks
+
+
+def finish_kernel(scale, shift, mine_ref, other_ref, states_ref, dev_ref, out_ref):
+    members, width = states_ref.shape
+    row = lax.broadcasted_iota(jnp.int32, (SUB, 2 * members), 0)
+    lane = lax.broadcasted_iota(jnp.int32, (SUB, 2 * members), 1)
+    blocks = []
+    for lo in range(0, members, SUB):
+        rows = slice(lo, lo + SUB)
+        block = (mine_ref[rows, :] + other_ref[rows, :]) * scale
+        blocks.append(block + jnp.where(lane == row + (members + lo), shift, 0.0))
+    solved = jnp.concatenate([b[:, :members] for b in eliminate(blocks, members)], axis=0)
+    mixing = solved.T.astype(jnp.bfloat16)
+    step = min(CHUNK, width)
+    for lo in range(0, width, step):
+        cols = slice(lo, lo + step)
+        move = jnp.dot(mixing, dev_ref[:, cols], preferred_element_type=jnp.float32)
+        out_ref[:, cols] = (states_ref[:, cols].astype(jnp.float32) + move).astype(jnp.bfloat16)
+
+
+def finish(scale, shift, mine, other, states, dev):
+    vmem = pl.BlockSpec(memory_space=pltpu.VMEM)
+    return pl.pallas_call(
+        lambda *refs: finish_kernel(scale, shift, *refs),
+        out_shape=jax.ShapeDtypeStruct(states.shape, jnp.bfloat16),
+        in_specs=[vmem] * 4,
+        out_specs=vmem,
+        compiler_params=pltpu.CompilerParams(vmem_limit_bytes=VMEM_LIMIT),
+        name="finish",
+    )(mine, other, states, dev)
+
+
+def finish_plain(scale, shift, mine, other, states, dev):
+    members = states.shape[0]
+    joined = (mine + other) * scale
+    kmat = joined[:, members:] + shift * jnp.eye(members, dtype=jnp.float32)
+    factor = jnp.linalg.cholesky(kmat)
+    middle = jax.scipy.linalg.solve_triangular(factor, joined[:, :members], lower=True)
+    solved = jax.scipy.linalg.solve_triangular(factor, middle, lower=True, trans="T")
+    mixing = solved.T.astype(jnp.bfloat16)
+    return (
+        states.astype(jnp.float32) + jnp.dot(mixing, dev, preferred_element_type=jnp.float32)
+    ).astype(jnp.bfloat16)
 
 
 def body(
@@ -75,16 +158,11 @@
     misfit = jnp.sum(resid_wide * resid_wide * prec_block)
     cross_t = contract(weighted, resid)
     eye = jnp.eye(member_total, dtype=jnp.float32)
-    joined = jnp.concatenate([gram + (misfit / member_total) * eye, cross_t], axis=1)
-    joined = total_over_devices(joined) / state_total
-    kmat = joined[:, :member_total] + 1e-06 * eye
-    factor = jnp.linalg.cholesky(kmat)
-    middle = jax.scipy.linalg.solve_triangular(factor, joined[:, member_total:], lower=True)
-    solved = jax.scipy.linalg.solve_triangular(factor, middle, lower=True, trans="T")
-    mixing = solved.T.astype(jnp.bfloat16)
-    fresh = (
-        state_wide + jnp.dot(mixing, state_dev, preferred_element_type=jnp.float32)
-    ).astype(jnp.bfloat16)
+    gram = 0.5 * (gram + gram.T)
+    joined = jnp.concatenate([cross_t, gram + (misfit / member_total) * eye], axis=1)
+    mine, other = total_over_devices(joined)
+    last = finish if member_total <= LANES // 2 and member_total % SUB == 0 else finish_plain
+    fresh = last(1.0 / state_total, 1e-06, mine, other, own_states, state_dev)
     return lax.all_to_all(fresh, "mem", split_axis=0, concat_axis=1, tiled=True)
 
 

time: 93.5 us -> 81.3 us (0.87)
  other arithmetic: 15.7 us -> 2.82 us
  Pallas kernels: 0 us -> 2.26 us
  local copies, waits for them, and re-layouts: 7.54 us -> 5.7 us
  waiting for transfers between devices: 30.1 us -> 31.5 us
    another operation x5 -> x0, other arithmetic: 12.1 us -> none  [the longest x3 6.52 us: body(): factor = jnp.linalg.cholesky(kmat)]
    pallas_call x0 -> x1, Pallas kernels: none -> 2.26 us  [finish(): pl.pallas_call(lambda *refs: finish_kernel(scale, shift, *refs), out_shap...]
    convert_element_type x2, local copies, waits for them, and re-layouts: 3.3 us -> 1.11 us  [body(): pred_wide = own_preds.astype(jnp.float32)]
    all_to_all x2, waiting for transfers between devices: 16.7 us -> 17.9 us  [to_block(): return lax.all_to_all(value, 'mem', split_axis=1, concat_axis=0, tiled=True)]
    unnamed x12 -> x8, local copies, waits for them, and re-layouts: 2.22 us -> 2.81 us
where the time goes in v2:
time: 81.3 us; the launch traced here: 80.8 us
  waiting for transfers between devices  31.5 us (39%)
  starting transfers between devices  17 us (21%)
  blocking collectives  14.5 us (18%)
  matrix products  6.13 us (8%)
  local copies, waits for them, and re-layouts  5.7 us (7%)
  other arithmetic  2.82 us (3%)
  Pallas kernels  2.26 us (3%)
  between operations  0.84 us (1%)
    all_to_all x2, waiting for transfers between devices, to_block(): return lax.all_to_all(value, 'mem', split_axis=1, concat_axis=0, tiled=True)  17.9 us
    all_to_all x1, blocking collectives, body(): return lax.all_to_all(fresh, 'mem', split_axis=0, concat_axis=1, tiled=True)  14.5 us
    ppermute x5, waiting for transfers between devices, total_over_devices(): other = lax.ppermute(value, axis, [(i, i ^ mask) for i in range(size)])  13.6 us
    all_to_all x2, starting transfers between devices, to_block(): return lax.all_to_all(value, 'mem', split_axis=1, concat_axis=0, tiled=True)  12.4 us
    dot_general x2, matrix products, forecast(): jnp.dot(hidden, exit_w[layer], preferred_element_type=jnp.float32)  5.23 us
    ppermute x5, starting transfers between devices, total_over_devices(): other = lax.ppermute(value, axis, [(i, i ^ mask) for i in range(size)])  4.61 us
    unnamed x8, local copies, waits for them, and re-layouts  2.81 us
    pallas_call x1, Pallas kernels, finish(): pl.pallas_call(lambda *refs: finish_kernel(scale, shift, *refs), out_shap...  2.26 us
  transfers between devices with their start and end apart: 7, of which 7 were waited for; matrix products, arithmetic and copies ran while one was open for 14% of the time, Pallas kernels for 0%

profile of v2, /device:TPU:0, one launch (start us, length us, event | category | flops | bytes accessed | tf_op | source)
XLA Modules:
  0.0 80.8 jit_solution(12859219654214431057)
XLA Ops:
  0.0 8.5 %all-to-all-start = ((bf16[4,16,4096]{2,0,1:T(4,128)(2,1)}), bf16[4,16,4096]{2,0,1:T(4,128)(2,1)S(1)}, u32[]{:S(2)}, u32[]{:S(2)}) async-start(bf16[4,16,4096]{2,0,1:T(4,128)(2,1)} %bitcast.70), calls=%async_computation | async-start | bytes 1048576 | tf_op jit(solution)/shard_map/all_to_all | solution.py:23
  8.5 0.7 dynamic_slice.3
  9.3 14.3 %all-to-all-done = bf16[4,16,4096]{2,0,1:T(4,128)(2,1)S(1)} async-done(((bf16[4,16,4096]{2,0,1:T(4,128)(2,1)}), bf16[4,16,4096]{2,0,1:T(4,128)(2,1)S(1)}, u32[]{:S(2)}, u32[]{:S(2)}) %all-to-all-start) | async-done | bytes 524320 | tf_op jit(solution)/shard_map/all_to_all | solution.py:23
  23.6 3.9 %all-to-all-start.1 = ((bf16[4,16,4096]{2,0,1:T(4,128)(2,1)}), bf16[4,16,4096]{2,0,1:T(4,128)(2,1)S(1)}, u32[]{:S(2)}, u32[]{:S(2)}) async-start(bf16[4,16,4096]{2,0,1:T(4,128)(2,1)} %bitcast.15), calls=%async_computation.1 | async-start | bytes 1048576 | tf_op jit(solution)/shard_map/all_to_all | solution.py:23
  27.5 0.4 reshape.68
  27.9 0.2 copy.13
  28.1 2.6 %fusion.2 = bf16[1024,256]{1,0:T(8,128)(2,1)S(1)} fusion(bf16[1024,256]{1,0:T(8,128)(2,1)S(1)} %bitcast.71, f32[1024]{0:T(1024)S(1)} %bitcast.73, f32[256]{0:T(256)S(1)} %bitcast.75, bf16[2,1024,256]{2,1,0:T(8,128)(2,1)} %param.12, bf16[2,256,1024]{2,1,0:T(8,128)(2,1)} %param.10), kind=kOutput, calls=%fused_computation.6 | convolution fusion | flops 1081081856 | bytes 2626560 | tf_op jit(solution)/shard_map/dot_general | solution.py:50
  30.7 2.6 %bitcast_convert_fusion = f32[16,64,256]{2,1,0:T(8,128)S(1)} fusion(f32[256]{0:T(256)S(1)} %bitcast.74, bf16[2,1024,256]{2,1,0:T(8,128)(2,1)} %param.12, bf16[1024,256]{1,0:T(8,128)(2,1)S(1)} %fusion.2, f32[1024]{0:T(1024)S(1)} %bitcast.72, bf16[2,256,1024]{2,1,0:T(8,128)(2,1)} %param.10), kind=kOutput, calls=%fused_computation.39 | convolution fusion | flops 1081344000 | bytes 3150848 | tf_op jit(solution)/shard_map/dot_general | solution.py:50
  33.3 0.6 copy.30
  33.9 0.5 fusion.23
  34.5 0.6 multiply_convert_fusion.2
  35.1 0.8 copy-done
  35.9 0.6 convolution_bitcast_fusion
  36.6 0.5 reshape.70
  37.1 1.2 %copy.19 = bf16[8,8,16,256]{3,1,2,0:T(8,128)(2,1)S(1)} copy(bf16[8,8,16,256]{3,2,1,0:T(8,128)(2,1)} %bitcast.69) | data formatting | bytes 1048576
  38.3 3.6 %all-to-all-done.1 = bf16[4,16,4096]{2,0,1:T(4,128)(2,1)S(1)} async-done(((bf16[4,16,4096]{2,0,1:T(4,128)(2,1)}), bf16[4,16,4096]{2,0,1:T(4,128)(2,1)S(1)}, u32[]{:S(2)}, u32[]{:S(2)}) %all-to-all-start.1) | async-done | bytes 524320 | tf_op jit(solution)/shard_map/all_to_all | solution.py:23
  41.9 1.2 %multiply_reduce_fusion = (f32[]{:T(128)}, bf16[16,4,4096]{2,1,0:T(4,128)(2,1)S(1)}) fusion(f32[4096]{0:T(1024)S(1)} %dynamic_slice.3, f32[16,4,4096]{2,1,0:T(4,128)S(1)} %reshape.70, bf16[4,16,4096]{2,0,1:T(4,128)(2,1)S(1)} %all-to-all-done.1), kind=kLoop, calls=%fused_computation.14 | loop fusion | flops 1835007 | bytes 2113540 | tf_op jit(solution)/shard_map/reduce_sum | solution.py:158
  43.9 0.3 fusion.27
  44.3 1.2 %collective-permute-done = f32[64,128]{1,0:T(8,128)S(1)} collective-permute-done((f32[64,128]{1,0:T(8,128)S(1)}, f32[64,128]{1,0:T(8,128)S(1)}, u32[]{:S(2)}, u32[]{:S(2)}) %collective-permute-start) | collective-permute-done | bytes 32800 | tf_op jit(solution)/shard_map/ppermute | solution.py:37
  45.6 0.6 collective-permute-start.1
  46.1 3.4 %collective-permute-done.1 = f32[64,128]{1,0:T(8,128)S(1)} collective-permute-done((f32[64,128]{1,0:T(8,128)S(1)}, f32[64,128]{1,0:T(8,128)S(1)}, u32[]{:S(2)}, u32[]{:S(2)}) %collective-permute-start.1) | collective-permute-done | bytes 32800 | tf_op jit(solution)/shard_map/ppermute | solution.py:37
  49.5 0.9 %collective-permute-start.2 = (f32[64,128]{1,0:T(8,128)S(1)}, f32[64,128]{1,0:T(8,128)S(1)}, u32[]{:S(2)}, u32[]{:S(2)}) collective-permute-start(f32[64,128]{1,0:T(8,128)S(1)} %add.94), channel_id=1, source_target_pairs={{0,4},{2,6},{4,0},{6,2},{8,12},{10,14},{12,8},{14,10},{16,20},{18,... | collective-permute-start | bytes 98312 | tf_op jit(solution)/shard_map/ppermute | solution.py:37
  50.4 0.2 convert_reduce_fusion
  50.6 2.8 %collective-permute-done.2 = f32[64,128]{1,0:T(8,128)S(1)} collective-permute-done((f32[64,128]{1,0:T(8,128)S(1)}, f32[64,128]{1,0:T(8,128)S(1)}, u32[]{:S(2)}, u32[]{:S(2)}) %collective-permute-start.2) | collective-permute-done | bytes 32800 | tf_op jit(solution)/shard_map/ppermute | solution.py:37
  53.4 1.3 %collective-permute-start.3 = (f32[64,128]{1,0:T(8,128)S(1)}, f32[64,128]{1,0:T(8,128)S(1)}, u32[]{:S(2)}, u32[]{:S(2)}) collective-permute-start(f32[64,128]{1,0:T(8,128)S(1)} %add.95), channel_id=1, source_target_pairs={{0,8},{2,10},{4,12},{6,14},{8,0},{10,2},{12,4},{14,6},{16,24},{18,... | collective-permute-start | bytes 98312 | tf_op jit(solution)/shard_map/ppermute | solution.py:37
  54.8 2.5 %collective-permute-done.3 = f32[64,128]{1,0:T(8,128)S(1)} collective-permute-done((f32[64,128]{1,0:T(8,128)S(1)}, f32[64,128]{1,0:T(8,128)S(1)}, u32[]{:S(2)}, u32[]{:S(2)}) %collective-permute-start.3) | collective-permute-done | bytes 32800 | tf_op jit(solution)/shard_map/ppermute | solution.py:37
  57.3 1.8 %collective-permute-start.4 = (f32[64,128]{1,0:T(8,128)S(1)}, f32[64,128]{1,0:T(8,128)S(1)}, u32[]{:S(2)}, u32[]{:S(2)}) collective-permute-start(f32[64,128]{1,0:T(8,128)S(1)} %add.96.refs_0_), channel_id=1, source_target_pairs={{0,24},{2,26},{4,28},{6,30},{8,16},{10,18},{12,20},{14,22},{16,8},... | collective-permute-start | bytes 98312 | tf_op jit(solution)/shard_map/ppermute | solution.py:37
  59.3 3.8 %collective-permute-done.4.refs_1_ = f32[64,128]{1,0:T(8,128)S(1)} collective-permute-done((f32[64,128]{1,0:T(8,128)S(1)}, f32[64,128]{1,0:T(8,128)S(1)}, u32[]{:S(2)}, u32[]{:S(2)}) %collective-permute-start.4) | collective-permute-done | bytes 32800 | tf_op jit(solution)/shard_map/ppermute | solution.py:37
  63.0 2.3 %finish.1 = bf16[64,4096]{1,0:T(8,128)(2,1)S(1)} custom-call(f32[64,128]{1,0:T(8,128)S(1)} %add.96.refs_0_, f32[64,128]{1,0:T(8,128)S(1)} %collective-permute-done.4.refs_1_, bf16[64,4096]{1,0:T(8,128)(2,1)S(1)} %all_to_all.43.refs_2_, bf16[64,4096]{1,0:T(8,128)(2,1)S(1)} %subtract_convert_fusion.refs_3_), custom_call_target="tpu_custom_call" | custom-call | tf_op jit(solution)/shard_map/finish/pallas_call | solution.py:108
  65.3 0.2 all_to_all.44
  65.5 14.5 %all_to_all.51 = bf16[16,4,4096]{2,1,0:T(4,128)(2,1)S(1)} all-to-all(bf16[16,4,4096]{2,1,0:T(4,128)(2,1)S(1)} %all_to_all.44), channel_id=1, replica_groups=mesh['mem'=16,'rep'=2] {'mem'}, dimensions={0} | all-to-all | bytes 1048576 | tf_op jit(solution)/shard_map/all_to_all | solution.py:166
  80.0 0.8 copy.32
  (21 shorter events, 0.6 us)
Async XLA Ops:
  0.0 9.2 %copy-start.2 = (f32[2,256]{1,0:T(2,128)S(1)}, f32[2,256]{1,0:T(2,128)}, u32[]{:S(2)}) copy-start(f32[2,256]{1,0:T(2,128)} %param.13) | copy-start | bytes 6148
  0.0 9.2 %copy-start.1 = (f32[2,1024]{1,0:T(2,128)S(1)}, f32[2,1024]{1,0:T(2,128)}, u32[]{:S(2)}) copy-start(f32[2,1024]{1,0:T(2,128)} %param.11) | copy-start | bytes 24580
  0.0 23.6 %all-to-all-start = ((bf16[4,16,4096]{2,0,1:T(4,128)(2,1)}), bf16[4,16,4096]{2,0,1:T(4,128)(2,1)S(1)}, u32[]{:S(2)}, u32[]{:S(2)}) async-start(bf16[4,16,4096]{2,0,1:T(4,128)(2,1)} %bitcast.70), calls=%async_computation | async-start | bytes 1048576 | tf_op jit(solution)/shard_map/all_to_all | solution.py:23
  23.6 18.4 %all-to-all-start.1 = ((bf16[4,16,4096]{2,0,1:T(4,128)(2,1)}), bf16[4,16,4096]{2,0,1:T(4,128)(2,1)S(1)}, u32[]{:S(2)}, u32[]{:S(2)}) async-start(bf16[4,16,4096]{2,0,1:T(4,128)(2,1)} %bitcast.15), calls=%async_computation.1 | async-start | bytes 1048576 | tf_op jit(solution)/shard_map/all_to_all | solution.py:23
  35.1 0.8 copy-start
  44.3 1.2 %collective-permute-start = (f32[64,128]{1,0:T(8,128)S(1)}, f32[64,128]{1,0:T(8,128)S(1)}, u32[]{:S(2)}, u32[]{:S(2)}) collective-permute-start(f32[64,128]{1,0:T(8,128)S(1)} %pad_maximum_fusion), channel_id=1, source_target_pairs={{0,1},{1,0},{2,3},{3,2},{4,5},{5,4},{6,7},{7,6},{8,9},{9,8},{10,11... | collective-permute-start | bytes 98312 | tf_op jit(solution)/shard_map/ppermute | solution.py:37
  45.6 3.9 %collective-permute-start.1 = (f32[64,128]{1,0:T(8,128)S(1)}, f32[64,128]{1,0:T(8,128)S(1)}, u32[]{:S(2)}, u32[]{:S(2)}) collective-permute-start(f32[64,128]{1,0:T(8,128)S(1)} %fusion.32), channel_id=1, source_target_pairs={{0,2},{2,0},{4,6},{6,4},{8,10},{10,8},{12,14},{14,12},{16,18},{18,... | collective-permute-start | bytes 98312 | tf_op jit(solution)/shard_map/ppermute | solution.py:37
  49.5 3.9 %collective-permute-start.2 = (f32[64,128]{1,0:T(8,128)S(1)}, f32[64,128]{1,0:T(8,128)S(1)}, u32[]{:S(2)}, u32[]{:S(2)}) collective-permute-start(f32[64,128]{1,0:T(8,128)S(1)} %add.94), channel_id=1, source_target_pairs={{0,4},{2,6},{4,0},{6,2},{8,12},{10,14},{12,8},{14,10},{16,20},{18,... | collective-permute-start | bytes 98312 | tf_op jit(solution)/shard_map/ppermute | solution.py:37
  53.4 3.9 %collective-permute-start.3 = (f32[64,128]{1,0:T(8,128)S(1)}, f32[64,128]{1,0:T(8,128)S(1)}, u32[]{:S(2)}, u32[]{:S(2)}) collective-permute-start(f32[64,128]{1,0:T(8,128)S(1)} %add.95), channel_id=1, source_target_pairs={{0,8},{2,10},{4,12},{6,14},{8,0},{10,2},{12,4},{14,6},{16,24},{18,... | collective-permute-start | bytes 98312 | tf_op jit(solution)/shard_map/ppermute | solution.py:37
  57.3 5.7 %collective-permute-start.4 = (f32[64,128]{1,0:T(8,128)S(1)}, f32[64,128]{1,0:T(8,128)S(1)}, u32[]{:S(2)}, u32[]{:S(2)}) collective-permute-start(f32[64,128]{1,0:T(8,128)S(1)} %add.96.refs_0_), channel_id=1, source_target_pairs={{0,24},{2,26},{4,28},{6,30},{8,16},{10,18},{12,20},{14,22},{16,8},... | collective-permute-start | bytes 98312 | tf_op jit(solution)/shard_map/ppermute | solution.py:37

commit v3 on v2

v3 whole, which is shorter than its diff:
```python
import jax
import jax.numpy as jnp
from jax import lax
from jax.experimental import pallas as pl
from jax.experimental.pallas import tpu as pltpu
from jax.sharding import PartitionSpec as P

PW = 256
LAYERS = 2
SUB = 8
LANES = 128
CHUNK = 512
VMEM_LIMIT = 8 * 1024 * 1024


def contract(left, right):
    return lax.dot_general(
        left, right, (((1,), (1,)), ((), ())), preferred_element_type=jnp.float32
    )


def halves(count):
    half = count // 2
    return [list(range(half)), [half + (i ^ (half // 2)) for i in range(half)]]


def to_block(value, groups):
    rows, _ = value.shape
    return lax.all_to_all(
        value.reshape(rows, len(groups[0]), -1),
        "mem", split_axis=1, concat_axis=0, axis_index_groups=groups,
    )


def mirror(value, groups):
    pairs = list(zip(*groups))
    return lax.ppermute(value, "mem", pairs + [(b, a) for a, b in pairs])


def total_over_half(value):
    count = lax.axis_size("mem")
    steps = [("rep", 2, 1)]
    bit = 1
    while bit < count // 2:
        steps.append(("mem", count, bit))
        bit *= 2
    other = jnp.zeros_like(value)
    for axis, size, mask in steps:
        value = value + other
        other = lax.ppermute(value, axis, [(i, i ^ mask) for i in range(size)])
    return value, other


def by_patch(value):
    rows, width = value.shape
    return value.reshape(rows, width // PW, PW).transpose(1, 0, 2).reshape(-1, PW)


def forecast_block(stream, layer, entry_w, entry_b, exit_w, exit_b):
    pre = jnp.dot(stream, entry_w[layer], preferred_element_type=jnp.float32) + entry_b[layer]
    hidden = jax.nn.silu(pre).astype(jnp.bfloat16)
    return (
        stream.astype(jnp.float32)
        + jnp.dot(hidden, exit_w[layer], preferred_element_type=jnp.float32)
        + exit_b[layer]
    ).astype(jnp.bfloat16)


def residual_kernel(obs_ref, own_ref, prec_ref, resid_ref, misfit_ref):
    patches = prec_ref.shape[0]
    rows = own_ref.shape[0] // patches
    total = jnp.zeros((rows, PW), jnp.float32)
    for p in range(patches):
        part = slice(p * rows, (p + 1) * rows)
        resid = (
            obs_ref[part, :].astype(jnp.float32) - own_ref[part, :].astype(jnp.float32)
        ).astype(jnp.bfloat16)
        resid_ref[part, :] = resid
        wide = resid.astype(jnp.float32)
        total = total + wide * wide * prec_ref[p : p + 1, :]
    misfit_ref[...] = jnp.full(misfit_ref.shape, jnp.sum(total))


def residual(obs, own, prec):
    vmem = pl.BlockSpec(memory_space=pltpu.VMEM)
    return pl.pallas_call(
        residual_kernel,
        out_shape=(
            jax.ShapeDtypeStruct(own.shape, jnp.bfloat16),
            jax.ShapeDtypeStruct((SUB, LANES), jnp.float32),
        ),
        in_specs=[vmem] * 3,
        out_specs=(vmem, vmem),
        compiler_params=pltpu.CompilerParams(vmem_limit_bytes=VMEM_LIMIT),
        name="residual",
    )(obs, own, prec)


def terms_kernel(own_ref, far_ref, resid_ref, prec_ref, share_ref, out_ref):
    patches = prec_ref.shape[0]
    rows = own_ref.shape[0] // patches
    members = 2 * rows
    cross = jnp.zeros((members, rows), jnp.float32)
    gram = jnp.zeros((members, members), jnp.float32)
    for p in range(patches):
        part = slice(p * rows, (p + 1) * rows)
        own = own_ref[part, :].astype(jnp.float32)
        far = far_ref[part, :].astype(jnp.float32)
        mean = (jnp.sum(own, axis=0, keepdims=True) + jnp.sum(far, axis=0, keepdims=True)) * (
            1.0 / members
        )
        dev = jnp.concatenate([own - mean, far - mean], axis=0).astype(jnp.bfloat16)
        weighted = (dev.astype(jnp.float32) * prec_ref[p : p + 1, :]).astype(jnp.bfloat16)
        cross = cross + contract(weighted, resid_ref[part, :])
        gram = gram + contract(weighted, dev)
    gram = 0.5 * (gram + gram.T)
    row = lax.broadcasted_iota(jnp.int32, (members, members), 0)
    col = lax.broadcasted_iota(jnp.int32, (members, members), 1)
    gram = gram + jnp.where(row == col, share_ref[0:1, 0:1], 0.0)
    out_ref[...] = jnp.concatenate([cross, jnp.zeros_like(cross), gram], axis=1)


def terms(own, far, resid, prec, share):
    patches = prec.shape[0]
    members = 2 * own.shape[0] // patches
    vmem = pl.BlockSpec(memory_space=pltpu.VMEM)
    return pl.pallas_call(
        terms_kernel,
        out_shape=jax.ShapeDtypeStruct((members, 2 * members), jnp.float32),
        in_specs=[vmem] * 5,
        out_specs=vmem,
        compiler_params=pltpu.CompilerParams(vmem_limit_bytes=VMEM_LIMIT),
        name="terms",
    )(own, far, resid, prec, share)


def terms_plain(own, far, resid, prec, share):
    patches = prec.shape[0]
    rows = own.shape[0] // patches
    members = 2 * rows

    def by_member(value):
        return value.reshape(patches, rows, PW).transpose(1, 0, 2).reshape(rows, patches * PW)

    preds = jnp.concatenate([by_member(own), by_member(far)], axis=0).astype(jnp.float32)
    dev = (preds - jnp.mean(preds, axis=0)).astype(jnp.bfloat16)
    weighted = (dev.astype(jnp.float32) * prec.reshape(-1)).astype(jnp.bfloat16)
    cross = contract(weighted, by_member(resid))
    gram = contract(weighted, dev)
    gram = 0.5 * (gram + gram.T) + share[0, 0] * jnp.eye(members, dtype=jnp.float32)
    return jnp.concatenate([cross, jnp.zeros_like(cross), gram], axis=1)


def eliminate(blocks, first):
    shape = blocks[0].shape
    row = lax.broadcasted_iota(jnp.int32, shape, 0)
    for kb in range(len(blocks)):
        lo = first + kb * SUB
        cols = [
            [jnp.broadcast_to(block[:, lo + j : lo + j + 1], shape) for j in range(SUB)]
            for block in blocks
        ]
        pivot = blocks[kb]
        own = list(cols[kb])
        for p in range(SUB):
            factor = own[p]
            inv = 1.0 / factor[p : p + 1, :]
            line = pivot[p : p + 1, :] * inv
            pivot = jnp.where(row == p, line, pivot - factor * line)
            for j in range(p + 1, SUB):
                line = own[j][p : p + 1, :] * inv
                own[j] = jnp.where(row == p, line, own[j] - factor * line)
        after = []
        for i, block in enumerate(blocks):
            if i == kb:
                after.append(pivot)
                continue
            terms = [cols[i][j] * pivot[j : j + 1, :] for j in range(SUB)]
            while len(terms) > 1:
                terms = [terms[t] + terms[t + 1] for t in range(0, len(terms), 2)]
            after.append(block - terms[0])
        blocks = after
    return blocks


def finish_kernel(scale, shift, mine_ref, other_ref, states_ref, dev_ref, out_ref):
    rows, width = states_ref.shape
    members = dev_ref.shape[0]
    row = lax.broadcasted_iota(jnp.int32, (SUB, 2 * members), 0)
    lane = lax.broadcasted_iota(jnp.int32, (SUB, 2 * members), 1)
    blocks = []
    for lo in range(0, members, SUB):
        part = slice(lo, lo + SUB)
        block = (mine_ref[part, :] + other_ref[part, :]) * scale
        blocks.append(block + jnp.where(lane == row + (members + lo), shift, 0.0))
    solved = jnp.concatenate([b[:, :members] for b in eliminate(blocks, members)], axis=0)
    mixing = solved.T[:rows, :].astype(jnp.bfloat16)
    step = min(CHUNK, width)
    for lo in range(0, width, step):
        cols = slice(lo, lo + step)
        move = jnp.dot(mixing, dev_ref[:, cols], preferred_element_type=jnp.float32)
        out_ref[:, cols] = (states_ref[:, cols].astype(jnp.float32) + move).astype(jnp.bfloat16)


def finish(scale, shift, mine, other, states, dev):
    vmem = pl.BlockSpec(memory_space=pltpu.VMEM)
    return pl.pallas_call(
        lambda *refs: finish_kernel(scale, shift, *refs),
        out_shape=jax.ShapeDtypeStruct(states.shape, jnp.bfloat16),
        in_specs=[vmem] * 4,
        out_specs=vmem,
        compiler_params=pltpu.CompilerParams(vmem_limit_bytes=VMEM_LIMIT),
        name="finish",
    )(mine, other, states, dev)


def finish_plain(scale, shift, mine, other, states, dev):
    rows, members = states.shape[0], dev.shape[0]
    joined = (mine + other) * scale
    kmat = joined[:, members:] + shift * jnp.eye(members, dtype=jnp.float32)
    factor = jnp.linalg.cholesky(kmat)
    middle = jax.scipy.linalg.solve_triangular(factor, joined[:, :rows], lower=True)
    solved = jax.scipy.linalg.solve_triangular(factor, middle, lower=True, trans="T")
    mixing = solved.T.astype(jnp.bfloat16)
    return (
        states.astype(jnp.float32) + jnp.dot(mixing, dev, preferred_element_type=jnp.float32)
    ).astype(jnp.bfloat16)


def body(
    particle_vectors,
    observed,
    precision,
    entry_projection_matrix,
    entry_offsets,
    exit_projection_matrix,
    exit_offsets,
):
    weights = (entry_projection_matrix, entry_offsets, exit_projection_matrix, exit_offsets)
    count = lax.axis_size("mem")
    if lax.axis_size("rep") != 2 or count < 4 or count & (count - 1):
        raise ValueError("unsupported mesh")
    groups = halves(count)
    state_total = particle_vectors.shape[1] * lax.axis_size("rep")
    member_total = particle_vectors.shape[0] * count
    own_states = to_block(particle_vectors, groups)
    far_states = mirror(own_states, groups)
    own_obs = to_block(observed, groups)
    width = own_states.shape[-1]
    own_states, far_states, own_obs = (
        v.reshape(-1, width) for v in (own_states, far_states, own_obs)
    )
    me = lax.axis_index("mem")
    place = jnp.where(me < count // 2, me, jnp.bitwise_xor(me - count // 2, count // 4))
    prec_block = lax.dynamic_slice_in_dim(precision, place * width, width).reshape(-1, PW)

    own_preds = by_patch(own_states)
    for layer in range(LAYERS):
        own_preds = forecast_block(own_preds, layer, *weights)
    resid, misfit = residual(by_patch(own_obs), own_preds, prec_block)
    far_preds = by_patch(far_states)
    for layer in range(LAYERS):
        far_preds = forecast_block(far_preds, layer, *weights)
        if layer == 0:
            far_preds, misfit = lax.optimization_barrier((far_preds, misfit))
    share = (misfit + mirror(misfit, groups)) * (1.0 / member_total)

    small = member_total <= LANES // 2 and member_total % (2 * SUB) == 0
    joined = (terms if small else terms_plain)(own_preds, far_preds, resid, prec_block, share)
    mine, other = total_over_half(joined)

    states = jnp.concatenate([own_states, far_states], axis=0).astype(jnp.float32)
    dev = (states - jnp.mean(states, axis=0)).astype(jnp.bfloat16)
    fresh = (finish if small else finish_plain)(
        1.0 / state_total, 1e-06, mine, other, own_states, dev
    )
    return lax.all_to_all(
        fresh, "mem", split_axis=0, concat_axis=1, tiled=True, axis_index_groups=groups
    )


def solution(mesh):
    placed = (P("mem", "rep"), P("mem", "rep"), P("rep"), P(), P(), P(), P())
    return jax.shard_map(
        body, mesh=mesh, in_specs=placed, out_specs=P("mem", "rep"), check_vma=False
    )
```

time: 81.3 us -> 83.3 us (1.025)
  waiting for transfers between devices: 31.5 us -> 16.2 us
  blocking collectives: 14.5 us -> 28.2 us
  matrix products: 6.13 us -> 11.6 us
  other arithmetic: 2.82 us -> 0.41 us
  local copies, waits for them, and re-layouts: 5.7 us -> 4 us
  starting transfers between devices: 17 us -> 18.6 us
  Pallas kernels: 2.26 us -> 3.54 us
    all_to_all x1 -> x2, blocking collectives: 14.5 us -> 28.2 us  [the longest x1 15.8 us: to_block(): lax.all_to_all(value.reshape(rows, len(groups[0]), -1), 'mem', split_axis...]
    all_to_all x2 -> x1, waiting for transfers between devices: 17.9 us -> 4.44 us  [to_block(): lax.all_to_all(value.reshape(rows, len(groups[0]), -1), 'mem', split_axis...]
    ppermute x5 -> x6, starting transfers between devices: 4.61 us -> 15.2 us  [the longest x2 10.6 us: mirror(): return lax.ppermute(value, 'mem', pairs + [(b, a) for a, b in pairs])]
    all_to_all x2 -> x1, starting transfers between devices: 12.4 us -> 3.5 us  [to_block(): lax.all_to_all(value.reshape(rows, len(groups[0]), -1), 'mem', split_axis...]
    dot_general x4, matrix products: 6.13 us -> 11.6 us  [forecast_block(): jnp.dot(hidden, exit_w[layer], preferred_element_type=jnp.float32)]
    unnamed x8 -> x5, local copies, waits for them, and re-layouts: 2.81 us -> 0.8 us
    ppermute x5 -> x6, waiting for transfers between devices: 13.6 us -> 11.8 us  [the longest x4 7.8 us: total_over_half(): other = lax.ppermute(value, axis, [(i, i ^ mask) for i in range(size)])]
    another operation x0 -> x6, local copies, waits for them, and re-layouts: none -> 1.8 us  [the longest x5 1.68 us: by_patch(): value.reshape(rows, width // PW, PW).transpose(1, 0, 2).reshape(-1, PW)]
  transfers between devices with their start and end apart: 7 -> 7, of which waited for: 7 -> 6; matrix products, arithmetic and copies ran while one was open for 14% -> 13% of each run, Pallas kernels for 0% -> 0%
where the time goes in v3:
time: 83.3 us; the launch traced here: 82.8 us
  blocking collectives  28.2 us (34%)
  starting transfers between devices  18.6 us (22%)
  waiting for transfers between devices  16.2 us (19%)
  matrix products  11.6 us (14%)
  local copies, waits for them, and re-layouts  4 us (5%)
  Pallas kernels  3.54 us (4%)
    all_to_all x1, blocking collectives, to_block(): lax.all_to_all(value.reshape(rows, len(groups[0]), -1), 'mem', split_axis...  15.8 us
    all_to_all x1, blocking collectives, body(): lax.all_to_all(fresh, 'mem', split_axis=0, concat_axis=1, tiled=True, axi...  12.4 us
    dot_general x4, matrix products, forecast_block(): jnp.dot(hidden, exit_w[layer], preferred_element_type=jnp.float32)  11.6 us
    ppermute x2, starting transfers between devices, mirror(): return lax.ppermute(value, 'mem', pairs + [(b, a) for a, b in pairs])  10.6 us
    ppermute x4, waiting for transfers between devices, total_over_half(): other = lax.ppermute(value, axis, [(i, i ^ mask) for i in range(size)])  7.8 us
    ppermute x4, starting transfers between devices, total_over_half(): other = lax.ppermute(value, axis, [(i, i ^ mask) for i in range(size)])  4.56 us
    all_to_all x1, waiting for transfers between devices, to_block(): lax.all_to_all(value.reshape(rows, len(groups[0]), -1), 'mem', split_axis...  4.44 us
    ppermute x2, waiting for transfers between devices, mirror(): return lax.ppermute(value, 'mem', pairs + [(b, a) for a, b in pairs])  3.97 us
  transfers between devices with their start and end apart: 7, of which 6 were waited for; matrix products, arithmetic and copies ran while one was open for 13% of the time, Pallas kernels for 0%

profile of v3, /device:TPU:0, one launch (start us, length us, event | category | flops | bytes accessed | tf_op | source)
XLA Modules:
  0.0 82.8 jit_solution(394628826318281912)
XLA Ops:
  0.0 15.8 %all_to_all.49 = bf16[1,4,8,8192]{3,1,0,2:T(4,128)(2,1)S(1)} all-to-all(bf16[1,4,8,8192]{3,1,0,2:T(4,128)(2,1)} %bitcast.68), channel_id=1, replica_groups={{0,2,4,6,8,10,12,14},{24,26,28,30,16,18,20,22},{1,3,5,7,9,11,13,15},{25..., dimensions={2} | all-to-all | bytes 1048576 | tf_op jit(solution)/shard_map/all_to_all | solution.py:29
  15.8 3.5 %all-to-all-start.1 = ((bf16[1,4,8,8192]{3,1,0,2:T(4,128)(2,1)}), bf16[1,4,8,8192]{3,1,0,2:T(4,128)(2,1)S(1)}, u32[]{:S(2)}, u32[]{:S(2)}) async-start(bf16[1,4,8,8192]{3,1,0,2:T(4,128)(2,1)} %bitcast.19), calls=%async_computation.1 | async-start | bytes 1048576 | tf_op jit(solution)/shard_map/all_to_all | solution.py:29
  19.3 0.8 dynamic_slice.3
  20.1 0.4 reshape_reshape_squeeze.6
  20.5 0.3 copy.18
  20.8 2.7 %collective-permute-start = (bf16[8,4,8192]{2,1,0:T(4,128)(2,1)S(1)}, bf16[8,4,8192]{2,1,0:T(4,128)(2,1)S(1)}, u32[]{:S(2)}, u32[]{:S(2)}) collective-permute-start(bf16[8,4,8192]{2,1,0:T(4,128)(2,1)S(1)} %bitcast.63), channel_id=1, source_target_pairs={{0,24},{2,26},{4,28},{6,30},{8,16},{10,18},{12,20},{14,22},{24,0},... | collective-permute-start | bytes 1572872 | tf_op jit(solution)/shard_map/ppermute | solution.py:37
  23.4 4.4 %all-to-all-done.1 = bf16[1,4,8,8192]{3,1,0,2:T(4,128)(2,1)S(1)} async-done(((bf16[1,4,8,8192]{3,1,0,2:T(4,128)(2,1)}), bf16[1,4,8,8192]{3,1,0,2:T(4,128)(2,1)S(1)}, u32[]{:S(2)}, u32[]{:S(2)}) %all-to-all-start.1) | async-done | bytes 524320 | tf_op jit(solution)/shard_map/all_to_all | solution.py:29
  27.9 0.4 reshape_reshape_squeeze.7
  28.2 0.3 copy.20
  28.5 2.6 %fusion.5 = bf16[1024,256]{1,0:T(8,128)(2,1)S(1)} fusion(bf16[1024,256]{1,0:T(8,128)(2,1)S(1)} %bitcast.69, f32[1024]{0:T(1024)S(1)} %bitcast.73, f32[256]{0:T(256)S(1)} %bitcast.77, bf16[2,1024,256]{2,1,0:T(8,128)(2,1)} %param.12, bf16[2,256,1024]{2,1,0:T(8,128)(2,1)} %param.10), kind=kOutput, calls=%fused_computation.14 | convolution fusion | flops 1081081856 | bytes 2626560 | tf_op jit(solution)/shard_map/dot_general | solution.py:64
  31.2 2.6 %fusion.6.own_ref = bf16[1024,256]{1,0:T(8,128)(2,1)S(1)} fusion(bf16[1024,256]{1,0:T(8,128)(2,1)S(1)} %fusion.5, f32[1024]{0:T(1024)S(1)} %bitcast.71, f32[256]{0:T(256)S(1)} %bitcast.75, bf16[2,1024,256]{2,1,0:T(8,128)(2,1)} %param.12, bf16[2,256,1024]{2,1,0:T(8,128)(2,1)} %param.10), kind=kOutput, calls=%fused_computation.15 | convolution fusion | flops 1081081856 | bytes 2626560 | tf_op jit(solution)/shard_map/dot_general | solution.py:64
  33.8 0.4 residual.1
  34.2 4.0 %collective-permute-done = bf16[8,4,8192]{2,1,0:T(4,128)(2,1)S(1)} collective-permute-done((bf16[8,4,8192]{2,1,0:T(4,128)(2,1)S(1)}, bf16[8,4,8192]{2,1,0:T(4,128)(2,1)S(1)}, u32[]{:S(2)}, u32[]{:S(2)}) %collective-permute-start) | collective-permute-done | bytes 524320 | tf_op jit(solution)/shard_map/ppermute | solution.py:37
  38.2 0.4 reshape_reshape.3
  38.5 0.3 copy.19
  38.8 3.4 %add_convert_fusion = bf16[1024,256]{1,0:T(8,128)(2,1)} fusion(bf16[1024,256]{1,0:T(8,128)(2,1)S(1)} %bitcast.70, f32[1024]{0:T(1024)S(1)} %bitcast.74, f32[256]{0:T(256)S(1)} %bitcast.78, bf16[2,1024,256]{2,1,0:T(8,128)(2,1)} %param.12, bf16[2,256,1024]{2,1,0:T(8,128)(2,1)} %param.10), kind=kOutput, calls=%fused_computation.18 | convolution fusion | flops 1081081856 | bytes 2626560 | tf_op jit(solution)/shard_map/dot_general | solution.py:64
  42.2 7.9 %collective-permute-start.1 = (f32[8,128]{1,0:T(8,128)S(1)}, f32[8,128]{1,0:T(8,128)S(1)}, u32[]{:S(2)}, u32[]{:S(2)}) collective-permute-start(f32[8,128]{1,0:T(8,128)S(1)} %get-tuple-element.12), channel_id=1, source_target_pairs={{0,24},{2,26},{4,28},{6,30},{8,16},{10,18},{12,20},{14,22},{24,0},... | collective-permute-start | bytes 12296 | tf_op jit(solution)/shard_map/ppermute | solution.py:37
  50.2 2.9 %fusion.7.far_ref = bf16[1024,256]{1,0:T(8,128)(2,1)S(1)} fusion(bf16[1024,256]{1,0:T(8,128)(2,1)} %add_convert_fusion, f32[1024]{0:T(1024)S(1)} %bitcast.72, f32[256]{0:T(256)S(1)} %bitcast.76, bf16[2,1024,256]{2,1,0:T(8,128)(2,1)} %param.12, bf16[2,256,1024]{2,1,0:T(8,128)(2,1)} %param.10), kind=kOutput, calls=%fused_computation.16 | convolution fusion | flops 1081081856 | bytes 2626560 | tf_op jit(solution)/shard_map/dot_general | solution.py:64
  53.1 0.9 %terms.1 = f32[64,128]{1,0:T(8,128)S(1)} custom-call(bf16[1024,256]{1,0:T(8,128)(2,1)S(1)} %fusion.6.own_ref, bf16[1024,256]{1,0:T(8,128)(2,1)S(1)} %fusion.7.far_ref, bf16[1024,256]{1,0:T(8,128)(2,1)S(1)} %get-tuple-element.11.resid_ref, f32[32,256]{1,0:T(8,128)S(1)} %reshape.28.prec_ref, f32[8,128]{1,0:T(8,128)S(1)} %add_multiply_fusion.share_ref), custom_call_target="tpu_custom_call" | custom-call | tf_op jit(solution)/shard_map/terms/pallas_call | solution.py:127
  54.4 0.9 %collective-permute-done.2 = f32[64,128]{1,0:T(8,128)S(1)} collective-permute-done((f32[64,128]{1,0:T(8,128)S(1)}, f32[64,128]{1,0:T(8,128)S(1)}, u32[]{:S(2)}, u32[]{:S(2)}) %collective-permute-start.2) | collective-permute-done | bytes 32800 | tf_op jit(solution)/shard_map/ppermute | solution.py:50
  55.3 1.5 %collective-permute-start.3 = (f32[64,128]{1,0:T(8,128)S(1)}, f32[64,128]{1,0:T(8,128)S(1)}, u32[]{:S(2)}, u32[]{:S(2)}) collective-permute-start(f32[64,128]{1,0:T(8,128)S(1)} %add.131), channel_id=1, source_target_pairs={{0,2},{2,0},{4,6},{6,4},{8,10},{10,8},{12,14},{14,12},{16,18},{18,... | collective-permute-start | bytes 98312 | tf_op jit(solution)/shard_map/ppermute | solution.py:50
  56.8 0.2 convert_reduce_fusion
  57.0 2.2 %collective-permute-done.3 = f32[64,128]{1,0:T(8,128)S(1)} collective-permute-done((f32[64,128]{1,0:T(8,128)S(1)}, f32[64,128]{1,0:T(8,128)S(1)}, u32[]{:S(2)}, u32[]{:S(2)}) %collective-permute-start.3) | collective-permute-done | bytes 32800 | tf_op jit(solution)/shard_map/ppermute | solution.py:50
  59.2 1.5 %collective-permute-start.4 = (f32[64,128]{1,0:T(8,128)S(1)}, f32[64,128]{1,0:T(8,128)S(1)}, u32[]{:S(2)}, u32[]{:S(2)}) collective-permute-start(f32[64,128]{1,0:T(8,128)S(1)} %add.132), channel_id=1, source_target_pairs={{0,4},{2,6},{4,0},{6,2},{8,12},{10,14},{12,8},{14,10},{16,20},{18,... | collective-permute-start | bytes 98312 | tf_op jit(solution)/shard_map/ppermute | solution.py:50
  60.7 2.4 %collective-permute-done.4 = f32[64,128]{1,0:T(8,128)S(1)} collective-permute-done((f32[64,128]{1,0:T(8,128)S(1)}, f32[64,128]{1,0:T(8,128)S(1)}, u32[]{:S(2)}, u32[]{:S(2)}) %collective-permute-start.4) | collective-permute-done | bytes 32800 | tf_op jit(solution)/shard_map/ppermute | solution.py:50
  63.1 1.5 %collective-permute-start.5 = (f32[64,128]{1,0:T(8,128)S(1)}, f32[64,128]{1,0:T(8,128)S(1)}, u32[]{:S(2)}, u32[]{:S(2)}) collective-permute-start(f32[64,128]{1,0:T(8,128)S(1)} %add.133.refs_0_), channel_id=1, source_target_pairs={{0,8},{2,10},{4,12},{6,14},{8,0},{10,2},{12,4},{14,6},{16,24},{18,... | collective-permute-start | bytes 98312 | tf_op jit(solution)/shard_map/ppermute | solution.py:50
  64.7 0.2 fusion.refs_3_
  64.9 2.2 %collective-permute-done.5.refs_1_ = f32[64,128]{1,0:T(8,128)S(1)} collective-permute-done((f32[64,128]{1,0:T(8,128)S(1)}, f32[64,128]{1,0:T(8,128)S(1)}, u32[]{:S(2)}, u32[]{:S(2)}) %collective-permute-start.5) | collective-permute-done | bytes 32800 | tf_op jit(solution)/shard_map/ppermute | solution.py:50
  67.1 2.3 %finish.1 = bf16[32,8192]{1,0:T(8,128)(2,1)S(1)} custom-call(f32[64,128]{1,0:T(8,128)S(1)} %add.133.refs_0_, f32[64,128]{1,0:T(8,128)S(1)} %collective-permute-done.5.refs_1_, bf16[32,8192]{1,0:T(8,128)(2,1)S(1)} %reshape_squeeze.3.refs_2_, bf16[64,8192]{1,0:T(8,128)(2,1)S(1)} %fusion.refs_3_), custom_call_target="tpu_custom_call" | custom-call | tf_op jit(solution)/shard_map/finish/pallas_call | solution.py:207
  69.3 0.2 all_to_all.42
  69.5 12.4 %all_to_all.50 = bf16[8,4,8192]{2,1,0:T(4,128)(2,1)S(1)} all-to-all(bf16[8,4,8192]{2,1,0:T(4,128)(2,1)S(1)} %all_to_all.42), channel_id=1, replica_groups={{0,2,4,6,8,10,12,14},{24,26,28,30,16,18,20,22},{1,3,5,7,9,11,13,15},{25..., dimensions={0} | all-to-all | bytes 1048576 | tf_op jit(solution)/shard_map/all_to_all | solution.py:277
  82.0 0.8 copy.23
  (16 shorter events, 0.4 us)
Async XLA Ops:
  0.0 20.1 %copy-start.1 = (f32[2,256]{1,0:T(2,128)S(1)}, f32[2,256]{1,0:T(2,128)}, u32[]{:S(2)}) copy-start(f32[2,256]{1,0:T(2,128)} %param.13) | copy-start | bytes 6148
  0.0 20.1 %copy-start = (f32[2,1024]{1,0:T(2,128)S(1)}, f32[2,1024]{1,0:T(2,128)}, u32[]{:S(2)}) copy-start(f32[2,1024]{1,0:T(2,128)} %param.11) | copy-start | bytes 24580
  15.8 12.1 %all-to-all-start.1 = ((bf16[1,4,8,8192]{3,1,0,2:T(4,128)(2,1)}), bf16[1,4,8,8192]{3,1,0,2:T(4,128)(2,1)S(1)}, u32[]{:S(2)}, u32[]{:S(2)}) async-start(bf16[1,4,8,8192]{3,1,0,2:T(4,128)(2,1)} %bitcast.19), calls=%async_computation.1 | async-start | bytes 1048576 | tf_op jit(solution)/shard_map/all_to_all | solution.py:29
  20.8 17.4 %collective-permute-start = (bf16[8,4,8192]{2,1,0:T(4,128)(2,1)S(1)}, bf16[8,4,8192]{2,1,0:T(4,128)(2,1)S(1)}, u32[]{:S(2)}, u32[]{:S(2)}) collective-permute-start(bf16[8,4,8192]{2,1,0:T(4,128)(2,1)S(1)} %bitcast.63), channel_id=1, source_target_pairs={{0,24},{2,26},{4,28},{6,30},{8,16},{10,18},{12,20},{14,22},{24,0},... | collective-permute-start | bytes 1572872 | tf_op jit(solution)/shard_map/ppermute | solution.py:37
  42.2 10.9 %collective-permute-start.1 = (f32[8,128]{1,0:T(8,128)S(1)}, f32[8,128]{1,0:T(8,128)S(1)}, u32[]{:S(2)}, u32[]{:S(2)}) collective-permute-start(f32[8,128]{1,0:T(8,128)S(1)} %get-tuple-element.12), channel_id=1, source_target_pairs={{0,24},{2,26},{4,28},{6,30},{8,16},{10,18},{12,20},{14,22},{24,0},... | collective-permute-start | bytes 12296 | tf_op jit(solution)/shard_map/ppermute | solution.py:37
  54.0 1.3 %collective-permute-start.2 = (f32[64,128]{1,0:T(8,128)S(1)}, f32[64,128]{1,0:T(8,128)S(1)}, u32[]{:S(2)}, u32[]{:S(2)}) collective-permute-start(f32[64,128]{1,0:T(8,128)S(1)} %terms.1), channel_id=1, source_target_pairs={{0,1},{1,0},{2,3},{3,2},{4,5},{5,4},{6,7},{7,6},{8,9},{9,8},{10,11... | collective-permute-start | bytes 98312 | tf_op jit(solution)/shard_map/ppermute | solution.py:50
  55.3 3.9 %collective-permute-start.3 = (f32[64,128]{1,0:T(8,128)S(1)}, f32[64,128]{1,0:T(8,128)S(1)}, u32[]{:S(2)}, u32[]{:S(2)}) collective-permute-start(f32[64,128]{1,0:T(8,128)S(1)} %add.131), channel_id=1, source_target_pairs={{0,2},{2,0},{4,6},{6,4},{8,10},{10,8},{12,14},{14,12},{16,18},{18,... | collective-permute-start | bytes 98312 | tf_op jit(solution)/shard_map/ppermute | solution.py:50
  59.2 3.9 %collective-permute-start.4 = (f32[64,128]{1,0:T(8,128)S(1)}, f32[64,128]{1,0:T(8,128)S(1)}, u32[]{:S(2)}, u32[]{:S(2)}) collective-permute-start(f32[64,128]{1,0:T(8,128)S(1)} %add.132), channel_id=1, source_target_pairs={{0,4},{2,6},{4,0},{6,2},{8,12},{10,14},{12,8},{14,10},{16,20},{18,... | collective-permute-start | bytes 98312 | tf_op jit(solution)/shard_map/ppermute | solution.py:50
  63.1 3.9 %collective-permute-start.5 = (f32[64,128]{1,0:T(8,128)S(1)}, f32[64,128]{1,0:T(8,128)S(1)}, u32[]{:S(2)}, u32[]{:S(2)}) collective-permute-start(f32[64,128]{1,0:T(8,128)S(1)} %add.133.refs_0_), channel_id=1, source_target_pairs={{0,8},{2,10},{4,12},{6,14},{8,0},{10,2},{12,4},{14,6},{16,24},{18,... | collective-permute-start | bytes 98312 | tf_op jit(solution)/shard_map/ppermute | solution.py:50

commit v4 on v3

--- a/solution.py
+++ b/solution.py
@@ -6,10 +6,10 @@
 from jax.sharding import PartitionSpec as P
 
 PW = 256
-LAYERS = 2
 SUB = 8
 LANES = 128
 CHUNK = 512
+ROWS = 512
 VMEM_LIMIT = 8 * 1024 * 1024
 
 
@@ -51,19 +51,54 @@
     return value, other
 
 
-def by_patch(value):
-    rows, width = value.shape
-    return value.reshape(rows, width // PW, PW).transpose(1, 0, 2).reshape(-1, PW)
-
-
-def forecast_block(stream, layer, entry_w, entry_b, exit_w, exit_b):
-    pre = jnp.dot(stream, entry_w[layer], preferred_element_type=jnp.float32) + entry_b[layer]
-    hidden = jax.nn.silu(pre).astype(jnp.bfloat16)
-    return (
-        stream.astype(jnp.float32)
-        + jnp.dot(hidden, exit_w[layer], preferred_element_type=jnp.float32)
-        + exit_b[layer]
-    ).astype(jnp.bfloat16)
+def rows_of(ref, at):
+    cols = slice(at, at + PW)
+    return jnp.concatenate(
+        [ref[s, :, cols].astype(jnp.float32) for s in range(ref.shape[0])], axis=0
+    )
+
+
+def forecast_kernel(x_ref, entry_ref, entry_b_ref, exit_ref, exit_b_ref, out_ref):
+    senders, few, width = x_ref.shape
+    rows = senders * few
+    layers, _, hid = entry_ref.shape
+    wide = min(ROWS, hid)
+    each = PW * max(1, ROWS // rows)
+    for first in range(0, width, each):
+        starts = range(first, min(first + each, width), PW)
+        stream = jnp.concatenate([rows_of(x_ref, at) for at in starts], axis=0)
+        stream = stream.astype(jnp.bfloat16)
+        for layer in range(layers):
+            acc = stream.astype(jnp.float32) + exit_b_ref[layer : layer + 1, :]
+            for at in range(0, hid, wide):
+                cols = slice(at, at + wide)
+                pre = jnp.dot(stream, entry_ref[layer, :, cols], preferred_element_type=jnp.float32)
+                pre = pre + entry_b_ref[layer : layer + 1, cols]
+                hidden = (pre * (0.5 * jnp.tanh(0.5 * pre) + 0.5)).astype(jnp.bfloat16)
+                acc = acc + jnp.dot(
+                    hidden, exit_ref[layer, cols, :], preferred_element_type=jnp.float32
+                )
+            stream = acc.astype(jnp.bfloat16)
+        lo = first // PW * rows
+        out_ref[lo : lo + stream.shape[0], :] = stream
+
+
+def forecast(stream, entry_w, entry_b, exit_w, exit_b):
+    vmem = pl.BlockSpec(memory_space=pltpu.VMEM)
+    work = stream.size // PW * entry_w.size
+    return pl.pallas_call(
+        forecast_kernel,
+        out_shape=jax.ShapeDtypeStruct((stream.size // PW, PW), jnp.bfloat16),
+        in_specs=[vmem] * 5,
+        out_specs=vmem,
+        cost_estimate=pl.CostEstimate(
+            flops=4 * work,
+            bytes_accessed=4 * (stream.size + entry_w.size),
+            transcendentals=work // PW,
+        ),
+        compiler_params=pltpu.CompilerParams(vmem_limit_bytes=2 * VMEM_LIMIT),
+        name="forecast",
+    )(stream, entry_w, entry_b, exit_w, exit_b)
 
 
 def residual_kernel(obs_ref, own_ref, prec_ref, resid_ref, misfit_ref):
@@ -73,7 +108,7 @@
     for p in range(patches):
         part = slice(p * rows, (p + 1) * rows)
         resid = (
-            obs_ref[part, :].astype(jnp.float32) - own_ref[part, :].astype(jnp.float32)
+            rows_of(obs_ref, p * PW) - own_ref[part, :].astype(jnp.float32)
         ).astype(jnp.bfloat16)
         resid_ref[part, :] = resid
         wide = resid.astype(jnp.float32)
@@ -247,28 +282,23 @@
     far_states = mirror(own_states, groups)
     own_obs = to_block(observed, groups)
     width = own_states.shape[-1]
-    own_states, far_states, own_obs = (
-        v.reshape(-1, width) for v in (own_states, far_states, own_obs)
-    )
+    rows = member_total // 2
     me = lax.axis_index("mem")
     place = jnp.where(me < count // 2, me, jnp.bitwise_xor(me - count // 2, count // 4))
     prec_block = lax.dynamic_slice_in_dim(precision, place * width, width).reshape(-1, PW)
 
-    own_preds = by_patch(own_states)
-    for layer in range(LAYERS):
-        own_preds = forecast_block(own_preds, layer, *weights)
-    resid, misfit = residual(by_patch(own_obs), own_preds, prec_block)
-    far_preds = by_patch(far_states)
-    for layer in range(LAYERS):
-        far_preds = forecast_block(far_preds, layer, *weights)
-        if layer == 0:
-            far_preds, misfit = lax.optimization_barrier((far_preds, misfit))
-    share = (misfit + mirror(misfit, groups)) * (1.0 / member_total)
+    own_preds = forecast(own_states, *weights)
+    resid, misfit = residual(own_obs, own_preds, prec_block)
+    far_misfit = mirror(misfit, groups)
+    far_preds = forecast(far_states, *weights)
+    share = (misfit + far_misfit) * (1.0 / member_total)
 
     small = member_total <= LANES // 2 and member_total % (2 * SUB) == 0
     joined = (terms if small else terms_plain)(own_preds, far_preds, resid, prec_block, share)
     mine, other = total_over_half(joined)
 
+    own_states = own_states.reshape(rows, width)
+    far_states = far_states.reshape(rows, width)
     states = jnp.concatenate([own_states, far_states], axis=0).astype(jnp.float32)
     dev = (states - jnp.mean(states, axis=0)).astype(jnp.bfloat16)
     fresh = (finish if small else finish_plain)(

time: 83.3 us -> 75.8 us (0.910)
  matrix products: 11.6 us -> 0 us
  waiting for transfers between devices: 16.2 us -> 10.2 us
  Pallas kernels: 3.54 us -> 9.12 us
  starting transfers between devices: 18.6 us -> 23.6 us
    dot_general x4 -> x0, matrix products: 11.6 us -> none  [forecast_block(): jnp.dot(hidden, exit_w[layer], preferred_element_type=jnp.float32)]
    pallas_call x0 -> x2, Pallas kernels: none -> 5.52 us  [forecast(): pl.pallas_call(forecast_kernel, out_shape=jax.ShapeDtypeStruct((stream.si...]
    ppermute x2, starting transfers between devices: 10.6 us -> 14.7 us  [mirror(): return lax.ppermute(value, 'mem', pairs + [(b, a) for a, b in pairs])]
    all_to_all x1, waiting for transfers between devices: 4.44 us -> 1.15 us  [to_block(): lax.all_to_all(value.reshape(rows, len(groups[0]), -1), 'mem', split_axis...]
    ppermute x2, waiting for transfers between devices: 3.97 us -> 1.69 us  [mirror(): return lax.ppermute(value, 'mem', pairs + [(b, a) for a, b in pairs])]
    another operation x6 -> x1, local copies, waits for them, and re-layouts: 1.8 us -> 0.12 us  [body(): own_states = own_states.reshape(rows, width)]
    unnamed x5 -> x11, local copies, waits for them, and re-layouts: 0.8 us -> 2.03 us
    ppermute x4, starting transfers between devices: 4.56 us -> 5.49 us  [total_over_half(): other = lax.ppermute(value, axis, [(i, i ^ mask) for i in range(size)])]
  transfers between devices with their start and end apart: 7 -> 7, of which waited for: 6 -> 6; matrix products, arithmetic and copies ran while one was open for 13% -> 2% of each run, Pallas kernels for 0% -> 4%
where the time goes in v4:
time: 75.8 us; the launch traced here: 75.4 us
  blocking collectives  28.7 us (38%)
  starting transfers between devices  23.6 us (31%)
  waiting for transfers between devices  10.2 us (13%)
  Pallas kernels  9.12 us (12%)
  local copies, waits for them, and re-layouts  3.23 us (4%)
    all_to_all x1, blocking collectives, to_block(): lax.all_to_all(value.reshape(rows, len(groups[0]), -1), 'mem', split_axis...  15.8 us
    ppermute x2, starting transfers between devices, mirror(): return lax.ppermute(value, 'mem', pairs + [(b, a) for a, b in pairs])  14.7 us
    all_to_all x1, blocking collectives, body(): lax.all_to_all(fresh, 'mem', split_axis=0, concat_axis=1, tiled=True, axi...  12.9 us
    ppermute x4, waiting for transfers between devices, total_over_half(): other = lax.ppermute(value, axis, [(i, i ^ mask) for i in range(size)])  7.32 us
    pallas_call x2, Pallas kernels, forecast(): pl.pallas_call(forecast_kernel, out_shape=jax.ShapeDtypeStruct((stream.si...  5.52 us
    ppermute x4, starting transfers between devices, total_over_half(): other = lax.ppermute(value, axis, [(i, i ^ mask) for i in range(size)])  5.49 us
    all_to_all x1, starting transfers between devices, to_block(): lax.all_to_all(value.reshape(rows, len(groups[0]), -1), 'mem', split_axis...  3.5 us
    pallas_call x1, Pallas kernels, finish(): pl.pallas_call(lambda *refs: finish_kernel(scale, shift, *refs), out_shap...  2.27 us
  transfers between devices with their start and end apart: 7, of which 6 were waited for; matrix products, arithmetic and copies ran while one was open for 2% of the time, Pallas kernels for 4%

profile of v4, /device:TPU:0, one launch (start us, length us, event | category | flops | bytes accessed | tf_op | source)
XLA Modules:
  0.0 75.4 jit_solution(3028695981185941391)
XLA Ops:
  0.0 15.8 %all_to_all.49 = bf16[1,4,8,8192]{3,1,0,2:T(4,128)(2,1)S(1)} all-to-all(bf16[1,4,8,8192]{3,1,0,2:T(4,128)(2,1)} %bitcast.22), channel_id=1, replica_groups={{0,2,4,6,8,10,12,14},{24,26,28,30,16,18,20,22},{1,3,5,7,9,11,13,15},{25..., dimensions={2} | all-to-all | bytes 1048576 | tf_op jit(solution)/shard_map/all_to_all | solution.py:29
  15.8 3.5 %all-to-all-start.1 = ((bf16[1,4,8,8192]{3,1,0,2:T(4,128)(2,1)}), bf16[1,4,8,8192]{3,1,0,2:T(4,128)(2,1)S(1)}, u32[]{:S(2)}, u32[]{:S(2)}) async-start(bf16[1,4,8,8192]{3,1,0,2:T(4,128)(2,1)} %bitcast.6), calls=%async_computation.1 | async-start | bytes 1048576 | tf_op jit(solution)/shard_map/all_to_all | solution.py:29
  19.3 2.7 %collective-permute-start = (bf16[8,4,8192]{2,1,0:T(4,128)(2,1)S(1)}, bf16[8,4,8192]{2,1,0:T(4,128)(2,1)S(1)}, u32[]{:S(2)}, u32[]{:S(2)}) collective-permute-start(bf16[8,4,8192]{2,1,0:T(4,128)(2,1)S(1)} %bitcast.17), channel_id=1, source_target_pairs={{0,24},{2,26},{4,28},{6,30},{8,16},{10,18},{12,20},{14,22},{24,0},... | collective-permute-start | bytes 1572872 | tf_op jit(solution)/shard_map/ppermute | solution.py:37
  21.9 0.8 %dynamic_slice.3 = f32[8192]{0:T(1024)S(1)} dynamic-slice(f32[65536]{0:T(1024)} %param.9, s32[]{:T(128)S(6)} %select_n.8), dynamic_slice_sizes={8192} | dynamic-slice | bytes 65540 | tf_op jit(solution)/shard_map/dynamic_slice | solution.py:288
  22.7 0.0 copy-done
  22.7 0.0 copy-done.3
  22.7 0.0 copy-start.1
  22.8 1.2 %copy-done.1 = bf16[2,1024,256]{2,1,0:T(8,128)(2,1)S(1)} copy-done((bf16[2,1024,256]{2,1,0:T(8,128)(2,1)S(1)}, bf16[2,1024,256]{2,1,0:T(8,128)(2,1)}, u32[]{:S(2)}) %copy-start.1) | copy-done | bytes 1048600
  24.0 2.8 %forecast.2.own_ref = bf16[1024,256]{1,0:T(8,128)(2,1)S(1)} custom-call(bf16[8,4,8192]{2,1,0:T(4,128)(2,1)S(1)} %bitcast.18, bf16[2,256,1024]{2,1,0:T(8,128)(2,1)S(1)} %copy-done, f32[2,1024]{1,0:T(2,128)S(1)} %copy-done.3, bf16[2,1024,256]{2,1,0:T(8,128)(2,1)S(1)} %copy-done.1, f32[2,256]{1,0:T(2,128)S(1)} %copy-done.4), custom_call_target="tpu_custom_call" | custom-call | flops 2147483648 | bytes 3145728 | tf_op jit(solution)/shard_map/forecast/pallas_call | solution.py:89
  26.7 1.1 %all-to-all-done.1 = bf16[1,4,8,8192]{3,1,0,2:T(4,128)(2,1)S(1)} async-done(((bf16[1,4,8,8192]{3,1,0,2:T(4,128)(2,1)}), bf16[1,4,8,8192]{3,1,0,2:T(4,128)(2,1)S(1)}, u32[]{:S(2)}, u32[]{:S(2)}) %all-to-all-start.1) | async-done | bytes 524320 | tf_op jit(solution)/shard_map/all_to_all | solution.py:29
  27.9 0.5 residual.1
  28.4 12.0 %collective-permute-start.1 = (f32[8,128]{1,0:T(8,128)S(1)}, f32[8,128]{1,0:T(8,128)S(1)}, u32[]{:S(2)}, u32[]{:S(2)}) collective-permute-start(f32[8,128]{1,0:T(8,128)S(1)} %get-tuple-element.8), channel_id=1, source_target_pairs={{0,24},{2,26},{4,28},{6,30},{8,16},{10,18},{12,20},{14,22},{24,0},... | collective-permute-start | bytes 12296 | tf_op jit(solution)/shard_map/ppermute | solution.py:37
  40.4 1.7 %collective-permute-done.1 = f32[8,128]{1,0:T(8,128)S(1)} collective-permute-done((f32[8,128]{1,0:T(8,128)S(1)}, f32[8,128]{1,0:T(8,128)S(1)}, u32[]{:S(2)}, u32[]{:S(2)}) %collective-permute-start.1) | collective-permute-done | bytes 4128 | tf_op jit(solution)/shard_map/ppermute | solution.py:37
  42.1 0.0 collective-permute-done.x_ref
  42.1 2.7 %forecast.3.far_ref = bf16[1024,256]{1,0:T(8,128)(2,1)S(1)} custom-call(bf16[8,4,8192]{2,1,0:T(4,128)(2,1)S(1)} %collective-permute-done.x_ref, bf16[2,256,1024]{2,1,0:T(8,128)(2,1)S(1)} %copy-done, f32[2,1024]{1,0:T(2,128)S(1)} %copy-done.3, bf16[2,1024,256]{2,1,0:T(8,128)(2,1)S(1)} %copy-done.2, f32[2,256]{1,0:T(2,128)S(1)} %copy-done.4), custom_call_target="tpu_custom_call" | custom-call | flops 2147483648 | bytes 3145728 | tf_op jit(solution)/shard_map/forecast/pallas_call | solution.py:89
  44.8 0.9 %terms.1 = f32[64,128]{1,0:T(8,128)S(1)} custom-call(bf16[1024,256]{1,0:T(8,128)(2,1)S(1)} %forecast.2.own_ref, bf16[1024,256]{1,0:T(8,128)(2,1)S(1)} %forecast.3.far_ref, bf16[1024,256]{1,0:T(8,128)(2,1)S(1)} %get-tuple-element.7.resid_ref, f32[32,256]{1,0:T(8,128)S(1)} %reshape.15.prec_ref, f32[8,128]{1,0:T(8,128)S(1)} %add_multiply_fusion.share_ref), custom_call_target="tpu_custom_call" | custom-call | tf_op jit(solution)/shard_map/terms/pallas_call | solution.py:162
  45.7 0.1 collective-permute-start.2
  45.8 0.1 reshape_squeeze.3.refs_2_
  45.9 0.1 reshape.16
  46.0 0.9 %collective-permute-done.2 = f32[64,128]{1,0:T(8,128)S(1)} collective-permute-done((f32[64,128]{1,0:T(8,128)S(1)}, f32[64,128]{1,0:T(8,128)S(1)}, u32[]{:S(2)}, u32[]{:S(2)}) %collective-permute-start.2) | collective-permute-done | bytes 32800 | tf_op jit(solution)/shard_map/ppermute | solution.py:50
  47.0 1.5 %collective-permute-start.3 = (f32[64,128]{1,0:T(8,128)S(1)}, f32[64,128]{1,0:T(8,128)S(1)}, u32[]{:S(2)}, u32[]{:S(2)}) collective-permute-start(f32[64,128]{1,0:T(8,128)S(1)} %add.18), channel_id=1, source_target_pairs={{0,2},{2,0},{4,6},{6,4},{8,10},{10,8},{12,14},{14,12},{16,18},{18,... | collective-permute-start | bytes 98312 | tf_op jit(solution)/shard_map/ppermute | solution.py:50
  48.5 0.2 convert_reduce_fusion
  48.6 2.3 %collective-permute-done.3 = f32[64,128]{1,0:T(8,128)S(1)} collective-permute-done((f32[64,128]{1,0:T(8,128)S(1)}, f32[64,128]{1,0:T(8,128)S(1)}, u32[]{:S(2)}, u32[]{:S(2)}) %collective-permute-start.3) | collective-permute-done | bytes 32800 | tf_op jit(solution)/shard_map/ppermute | solution.py:50
  50.9 1.5 %collective-permute-start.4 = (f32[64,128]{1,0:T(8,128)S(1)}, f32[64,128]{1,0:T(8,128)S(1)}, u32[]{:S(2)}, u32[]{:S(2)}) collective-permute-start(f32[64,128]{1,0:T(8,128)S(1)} %add.19), channel_id=1, source_target_pairs={{0,4},{2,6},{4,0},{6,2},{8,12},{10,14},{12,8},{14,10},{16,20},{18,... | collective-permute-start | bytes 98312 | tf_op jit(solution)/shard_map/ppermute | solution.py:50
  52.4 2.4 %collective-permute-done.4 = f32[64,128]{1,0:T(8,128)S(1)} collective-permute-done((f32[64,128]{1,0:T(8,128)S(1)}, f32[64,128]{1,0:T(8,128)S(1)}, u32[]{:S(2)}, u32[]{:S(2)}) %collective-permute-start.4) | collective-permute-done | bytes 32800 | tf_op jit(solution)/shard_map/ppermute | solution.py:50
  54.8 2.5 %collective-permute-start.5 = (f32[64,128]{1,0:T(8,128)S(1)}, f32[64,128]{1,0:T(8,128)S(1)}, u32[]{:S(2)}, u32[]{:S(2)}) collective-permute-start(f32[64,128]{1,0:T(8,128)S(1)} %add.20.refs_0_), channel_id=1, source_target_pairs={{0,8},{2,10},{4,12},{6,14},{8,0},{10,2},{12,4},{14,6},{16,24},{18,... | collective-permute-start | bytes 98312 | tf_op jit(solution)/shard_map/ppermute | solution.py:50
  57.3 0.2 fusion.refs_3_
  57.5 1.7 %collective-permute-done.5.refs_1_ = f32[64,128]{1,0:T(8,128)S(1)} collective-permute-done((f32[64,128]{1,0:T(8,128)S(1)}, f32[64,128]{1,0:T(8,128)S(1)}, u32[]{:S(2)}, u32[]{:S(2)}) %collective-permute-start.5) | collective-permute-done | bytes 32800 | tf_op jit(solution)/shard_map/ppermute | solution.py:50
  59.2 2.3 %finish.1 = bf16[32,8192]{1,0:T(8,128)(2,1)S(1)} custom-call(f32[64,128]{1,0:T(8,128)S(1)} %add.20.refs_0_, f32[64,128]{1,0:T(8,128)S(1)} %collective-permute-done.5.refs_1_, bf16[32,8192]{1,0:T(8,128)(2,1)S(1)} %reshape_squeeze.3.refs_2_, bf16[64,8192]{1,0:T(8,128)(2,1)S(1)} %fusion.refs_3_), custom_call_target="tpu_custom_call" | custom-call | tf_op jit(solution)/shard_map/finish/pallas_call | solution.py:242
  61.5 0.2 all_to_all.42
  61.7 12.9 %all_to_all.50 = bf16[8,4,8192]{2,1,0:T(4,128)(2,1)S(1)} all-to-all(bf16[8,4,8192]{2,1,0:T(4,128)(2,1)S(1)} %all_to_all.42), channel_id=1, replica_groups={{0,2,4,6,8,10,12,14},{24,26,28,30,16,18,20,22},{1,3,5,7,9,11,13,15},{25..., dimensions={0} | all-to-all | bytes 1048576 | tf_op jit(solution)/shard_map/all_to_all | solution.py:307
  74.6 0.8 %copy.11 = bf16[4,65536]{1,0:T(4,128)(2,1)} copy(bf16[4,65536]{1,0:T(4,128)(2,1)S(1)} %bitcast.21) | data formatting | bytes 1048576
  (12 shorter events, 0.0 us)
Async XLA Ops:
  0.0 22.7 %copy-start = (bf16[2,256,1024]{2,1,0:T(8,128)(2,1)S(1)}, bf16[2,256,1024]{2,1,0:T(8,128)(2,1)}, u32[]{:S(2)}) copy-start(bf16[2,256,1024]{2,1,0:T(8,128)(2,1)} %entry_ref.3) | copy-start | bytes 3145732
  0.0 22.7 %copy-start.3 = (f32[2,1024]{1,0:T(2,128)S(1)}, f32[2,1024]{1,0:T(2,128)}, u32[]{:S(2)}) copy-start(f32[2,1024]{1,0:T(2,128)} %entry_b_ref.3) | copy-start | bytes 24580
  0.0 22.7 %copy-start.4 = (f32[2,256]{1,0:T(2,128)S(1)}, f32[2,256]{1,0:T(2,128)}, u32[]{:S(2)}) copy-start(f32[2,256]{1,0:T(2,128)} %exit_b_ref.3) | copy-start | bytes 6148
  15.8 12.1 %all-to-all-start.1 = ((bf16[1,4,8,8192]{3,1,0,2:T(4,128)(2,1)}), bf16[1,4,8,8192]{3,1,0,2:T(4,128)(2,1)S(1)}, u32[]{:S(2)}, u32[]{:S(2)}) async-start(bf16[1,4,8,8192]{3,1,0,2:T(4,128)(2,1)} %bitcast.6), calls=%async_computation.1 | async-start | bytes 1048576 | tf_op jit(solution)/shard_map/all_to_all | solution.py:29
  19.3 22.8 %collective-permute-start = (bf16[8,4,8192]{2,1,0:T(4,128)(2,1)S(1)}, bf16[8,4,8192]{2,1,0:T(4,128)(2,1)S(1)}, u32[]{:S(2)}, u32[]{:S(2)}) collective-permute-start(bf16[8,4,8192]{2,1,0:T(4,128)(2,1)S(1)} %bitcast.17), channel_id=1, source_target_pairs={{0,24},{2,26},{4,28},{6,30},{8,16},{10,18},{12,20},{14,22},{24,0},... | collective-permute-start | bytes 1572872 | tf_op jit(solution)/shard_map/ppermute | solution.py:37
  22.7 1.2 %copy-start.1 = (bf16[2,1024,256]{2,1,0:T(8,128)(2,1)S(1)}, bf16[2,1024,256]{2,1,0:T(8,128)(2,1)}, u32[]{:S(2)}) copy-start(bf16[2,1024,256]{2,1,0:T(8,128)(2,1)} %exit_ref.3) | copy-start | bytes 3145732
  27.9 14.2 %copy-start.2 = (bf16[2,1024,256]{2,1,0:T(8,128)(2,1)S(1)}, bf16[2,1024,256]{2,1,0:T(8,128)(2,1)}, u32[]{:S(2)}) copy-start(bf16[2,1024,256]{2,1,0:T(8,128)(2,1)} %exit_ref.3) | copy-start | bytes 3145732
  28.4 13.7 %collective-permute-start.1 = (f32[8,128]{1,0:T(8,128)S(1)}, f32[8,128]{1,0:T(8,128)S(1)}, u32[]{:S(2)}, u32[]{:S(2)}) collective-permute-start(f32[8,128]{1,0:T(8,128)S(1)} %get-tuple-element.8), channel_id=1, source_target_pairs={{0,24},{2,26},{4,28},{6,30},{8,16},{10,18},{12,20},{14,22},{24,0},... | collective-permute-start | bytes 12296 | tf_op jit(solution)/shard_map/ppermute | solution.py:37
  45.7 1.3 %collective-permute-start.2 = (f32[64,128]{1,0:T(8,128)S(1)}, f32[64,128]{1,0:T(8,128)S(1)}, u32[]{:S(2)}, u32[]{:S(2)}) collective-permute-start(f32[64,128]{1,0:T(8,128)S(1)} %terms.1), channel_id=1, source_target_pairs={{0,1},{1,0},{2,3},{3,2},{4,5},{5,4},{6,7},{7,6},{8,9},{9,8},{10,11... | collective-permute-start | bytes 98312 | tf_op jit(solution)/shard_map/ppermute | solution.py:50
  47.0 3.9 %collective-permute-start.3 = (f32[64,128]{1,0:T(8,128)S(1)}, f32[64,128]{1,0:T(8,128)S(1)}, u32[]{:S(2)}, u32[]{:S(2)}) collective-permute-start(f32[64,128]{1,0:T(8,128)S(1)} %add.18), channel_id=1, source_target_pairs={{0,2},{2,0},{4,6},{6,4},{8,10},{10,8},{12,14},{14,12},{16,18},{18,... | collective-permute-start | bytes 98312 | tf_op jit(solution)/shard_map/ppermute | solution.py:50
  50.9 3.9 %collective-permute-start.4 = (f32[64,128]{1,0:T(8,128)S(1)}, f32[64,128]{1,0:T(8,128)S(1)}, u32[]{:S(2)}, u32[]{:S(2)}) collective-permute-start(f32[64,128]{1,0:T(8,128)S(1)} %add.19), channel_id=1, source_target_pairs={{0,4},{2,6},{4,0},{6,2},{8,12},{10,14},{12,8},{14,10},{16,20},{18,... | collective-permute-start | bytes 98312 | tf_op jit(solution)/shard_map/ppermute | solution.py:50
  54.8 4.4 %collective-permute-start.5 = (f32[64,128]{1,0:T(8,128)S(1)}, f32[64,128]{1,0:T(8,128)S(1)}, u32[]{:S(2)}, u32[]{:S(2)}) collective-permute-start(f32[64,128]{1,0:T(8,128)S(1)} %add.20.refs_0_), channel_id=1, source_target_pairs={{0,8},{2,10},{4,12},{6,14},{8,0},{10,2},{12,4},{14,6},{16,24},{18,... | collective-permute-start | bytes 98312 | tf_op jit(solution)/shard_map/ppermute | solution.py:50
